TPU v7x, 512 devices: a whole 4x8x8 slice. The times are simulated.
512 devices in a mesh: enc: 16 (over y, x_lo), slab: 32 (over x_hi, z, core).
Axes of the slice: x: 4 (x_hi: 2, x_lo: 2; x = x_hi * 2 + x_lo), y: 8, z: 8, core: 2. Of those that a mesh axis runs over, the one named last changes fastest.
Arguments:
- tokens: bfloat16 [32768, 1024], P(('slab', 'enc')), may hold values from -6 to 6
- cotangent: bfloat16 [32768, 1024], P(('slab', 'enc')), may hold values from -6 to 6
- w_qkv: bfloat16 [1024, 3072], P('slab', 'enc'), may hold values from -0.5 to 0.5
- w_out: bfloat16 [1024, 1024], P('enc', 'slab'), may hold values from -0.1875 to 0.1875
- mod_scale: float32 [1024], replicated, may hold values from -0.5 to 0.5
- mod_shift: float32 [1024], replicated, may hold values from -0.5 to 0.5
- mod_gate: float32 [1024], replicated, may hold values from 0.5 to 1.5
- counts: int32 [64], P('slab'), may hold values from 64 to 512
- edge_index: int32 [64, 128], P('slab'), may hold values from 0 to 1023
Outputs:
- grad_tokens: bfloat16 [32768, 1024], P(('slab', 'enc'))
- grad_qkv: float32 [1024, 3072], P('slab', 'enc')
- grad_out: float32 [1024, 1024], P('enc', 'slab')
Inputs may be any that keep to these rules, and one draw needn't show every extreme that they name: The first counts[w] slots of window w hold voxels; the rest are padding. `edge_index`: A row index within the preceding slab's 2 * 512 rows.
All inputs are finite; a program needn't handle non-finite values.
Results may differ from a plain program's by a relative error of at most 0.023.
Values may be sent and summed in bfloat16 or wider, within the bound.
A program may use at most 64 MiB of HBM per device.

v0:
```python
import jax
import jax.numpy as jnp
from jax import lax
from jax.sharding import PartitionSpec as P

HD = 64


EPS = 1e-06


def in_one_piece(arrays, axis, dim, along):
    widths = [a.shape[along] for a in arrays]
    both = jnp.concatenate(arrays, axis=along)
    whole = lax.all_gather(both, axis, axis=dim, tiled=True)
    return tuple(jnp.split(whole, [sum(widths[:k]) for k in range(1, len(widths))], axis=along))


def turned_gather(arrays, axis, dims):
    turned = [jnp.moveaxis(a, dim, 0) for a, dim in zip(arrays, dims)]
    widths = [t[0].size for t in turned]
    both = jnp.concatenate([t.reshape(-1, w) for t, w in zip(turned, widths)], axis=1)
    whole = lax.all_gather(both, axis, axis=0, tiled=True)
    blocks = jnp.split(whole, [sum(widths[:k]) for k in range(1, len(widths))], axis=1)
    return tuple(
        (
            jnp.moveaxis(b.reshape(-1, *t.shape[1:]), 0, dim)
            for b, t, dim in zip(blocks, turned, dims)
        )
    )


def shifted(block, axis, distance):
    devices = range(lax.axis_size(axis))
    route = [(i - distance, i) for i in devices if i - distance in devices]
    return lax.ppermute(block, axis, route)


def in_blocks(array, dim, peers):
    before, after = (array.shape[:dim], array.shape[dim + 1 :])
    return jnp.moveaxis(array.reshape(*before, peers, -1, *after), dim, 0)


def sum_at_owner(array, axis, dim):
    blocks = in_blocks(array, dim, lax.axis_size(axis))
    arrived = lax.all_to_all(blocks, axis, split_axis=0, concat_axis=0, tiled=True)
    return arrived.astype(jnp.float32).sum(axis=0)


def statistics(features):
    widened = features.astype(jnp.float32)
    average = jnp.mean(widened, 1, keepdims=True)
    centred = widened - average
    variance = jnp.mean(centred * centred, 1, keepdims=True)
    inv_std = lax.rsqrt(variance + EPS)
    return (centred * inv_std, inv_std)


def attend(query, key_vals, edge_vals, counts, edge_live, upstream, out_rows):
    windows = counts.shape[0]
    row_count = query.shape[0]
    win_size = row_count // windows
    head_size = query.shape[1]
    factor = head_size ** (-0.5)
    query_win = query.reshape(windows, win_size, head_size)
    keys_all = jnp.concatenate([key_vals.reshape(windows, win_size, 2 * head_size), edge_vals], 1)
    key_part = keys_all[:, :, :head_size]
    value_part = keys_all[:, :, head_size:]
    position = jnp.arange(win_size, dtype=jnp.int32)
    own_live = position[None, :] < counts[:, None]
    key_live = jnp.concatenate(
        [own_live, jnp.broadcast_to(edge_live[:, None], (windows, edge_vals.shape[1]))], 1
    )
    row_live = own_live.astype(jnp.float32)[:, :, None]
    scores = (
        jnp.einsum("wqd,wkd->wqk", query_win, key_part, preferred_element_type=jnp.float32) * factor
    )
    scores = jnp.where(key_live[:, None, :], scores, -1000000000.0)
    largest = jnp.max(scores, -1, keepdims=True)
    exponent = jnp.exp(scores - largest)
    softmax_p = exponent / jnp.sum(exponent, -1, keepdims=True)
    weights_b = softmax_p.astype(jnp.bfloat16)
    attended = (
        jnp.einsum("wqk,wkd->wqd", weights_b, value_part, preferred_element_type=jnp.float32)
        * row_live
    )
    attended = attended.astype(jnp.bfloat16).reshape(row_count, head_size)
    grad_att = jnp.dot(upstream, out_rows.T, preferred_element_type=jnp.float32).reshape(
        windows, win_size, head_size
    )
    grad_att = (grad_att * row_live).astype(jnp.bfloat16)
    grad_prob = jnp.einsum("wqd,wkd->wqk", grad_att, value_part, preferred_element_type=jnp.float32)
    grad_value = jnp.einsum("wqk,wqd->wkd", weights_b, grad_att, preferred_element_type=jnp.float32)
    grad_score = (
        softmax_p * (grad_prob - jnp.sum(grad_prob * softmax_p, -1, keepdims=True)) * factor
    )
    grad_score = grad_score.astype(jnp.bfloat16)
    grad_query = jnp.einsum(
        "wqk,wkd->wqd", grad_score, key_part, preferred_element_type=jnp.float32
    )
    grad_key = jnp.einsum("wqk,wqd->wkd", grad_score, query_win, preferred_element_type=jnp.float32)
    grad_pair = jnp.concatenate([grad_key, grad_value], -1)
    own_pair = grad_pair[:, :win_size].reshape(row_count, 2 * head_size)
    return (attended, grad_query.reshape(row_count, head_size), own_pair, grad_pair[:, win_size:])


def on_device(tokens, cotangent, w_qkv, w_out, mod_scale, mod_shift, mod_gate, counts, edge_index):
    features, upstream_in = in_one_piece((tokens, cotangent), "enc", 0, 1)
    weight_in, weight_out = turned_gather((w_qkv, w_out), "slab", (0, 1))
    normal_x, inv_std = statistics(features)
    gain = 1.0 + mod_scale
    normed = (normal_x * gain + mod_shift).astype(jnp.bfloat16)
    upstream = (upstream_in.astype(jnp.float32) * mod_gate).astype(jnp.bfloat16)
    windows = counts.shape[0]
    edge_count = edge_index.shape[1]
    heads_here = weight_out.shape[0] // HD
    pair_width = 2 * HD
    projected = jnp.dot(normed, weight_in, preferred_element_type=jnp.float32).astype(jnp.bfloat16)
    key_vals = projected[:, HD : 3 * HD]
    slab_index = lax.axis_index("slab")
    edge_live = jnp.full((windows,), slab_index > 0)
    flat_index = edge_index.reshape(-1)
    next_index = shifted(flat_index, "slab", -1)
    picked = jnp.take(key_vals, next_index, axis=0)
    edge_vals = shifted(picked, "slab", 1)
    edge_vals = edge_vals.reshape(windows, edge_count, heads_here * pair_width)
    attended, grad_query, own_pair, edge_pair = attend(
        projected[:, :HD], projected[:, HD:], edge_vals, counts, edge_live, upstream, weight_out
    )
    own_grads = own_pair
    edge_grads = edge_pair.reshape(-1, heads_here * pair_width)
    returned = shifted(edge_grads.astype(jnp.bfloat16), "slab", -1).astype(edge_grads.dtype)
    own_grads = own_grads.at[next_index].add(returned)
    grad_proj = jnp.concatenate([grad_query, own_grads], 1).astype(jnp.bfloat16)
    grad_q_local = jnp.dot(normed.T, grad_proj, preferred_element_type=jnp.float32)
    grad_o_local = jnp.dot(attended.T, upstream, preferred_element_type=jnp.float32)
    partial_value = jnp.dot(grad_proj, weight_in.T, preferred_element_type=jnp.float32)
    own_rows = tokens.shape[0]
    row_start = lax.axis_index("enc") * own_rows
    normal_own = lax.dynamic_slice_in_dim(normal_x, row_start, own_rows, 0)
    inv_own = lax.dynamic_slice_in_dim(inv_std, row_start, own_rows, 0)
    mine = sum_at_owner(partial_value.astype(jnp.bfloat16), "enc", 0)
    grad_hat = mine * gain
    grad_tokens = cotangent.astype(jnp.float32) + inv_own * (
        grad_hat
        - jnp.mean(grad_hat, 1, keepdims=True)
        - normal_own * jnp.mean(grad_hat * normal_own, 1, keepdims=True)
    )
    grad_qkv, grad_out = (
        sum_at_owner(grad_q_local.astype(jnp.bfloat16), "slab", 0),
        sum_at_owner(grad_o_local.astype(jnp.bfloat16), "slab", 1),
    )
    return (grad_tokens.astype(jnp.bfloat16), grad_qkv, grad_out)


def solution(mesh):
    placed = (
        P(("slab", "enc"), None),
        P(("slab", "enc"), None),
        P("slab", "enc"),
        P("enc", "slab"),
        P(),
        P(),
        P(),
        P("slab"),
        P("slab", None),
    )
    return jax.shard_map(
        on_device,
        mesh=mesh,
        in_specs=placed,
        out_specs=(P(("slab", "enc"), None), P("slab", "enc"), P("enc", "slab")),
        check_vma=False,
    )
```

profile of v0, /device:TPU:1, one launch (start us, length us, event | category | flops | bytes accessed | tf_op | source)
XLA Modules:
  0.0 279.5 jit_solution(14782367953100508507)
XLA Ops:
  7.2 0.0 all-gather.2.cloned.1.call-start
  7.2 1.7 pad_maximum_fusion.3
  8.9 0.0 all-gather.2.cloned.1.call-update
  8.9 8.7 %collective-permute-start = (s32[256]{0:T(256)}, s32[256]{0:T(256)S(1)}, u32[]{:S(2)}, u32[]{:S(2)}) collective-permute-start(s32[256]{0:T(256)} %bitcast.70), channel_id=1, source_target_pairs={{1,0},{2,1},{3,2},{4,3},{5,4},{6,5},{7,6},{8,7},{9,8},{10,9},{11,1... | collective-permute-start | bytes 3080 | tf_op jit(solution)/shard_map/ppermute | solution.py:36
  17.7 0.8 pad_maximum_fusion.8
  18.5 0.7 broadcast_add_fusion
  19.2 44.5 %all_gather.7 = bf16[1024,256]{1,0:T(8,128)(2,1)S(1)} all-gather(bf16[32,256]{1,0:T(8,128)(2,1)S(1)} %pad_maximum_fusion.8), channel_id=1, replica_groups=mesh['enc'=16,'slab'=32] {'slab'}, dimensions={0}, use_global_device_ids=true | all-gather | bytes 540672 | tf_op jit(solution)/shard_map/all_gather | solution.py:23
  63.7 0.7 iota_compare_fusion
  64.5 0.6 concatenate.20
  65.0 0.0 collective-permute-done
  65.1 53.5 %all-gather.2.cloned.1.call-done = bf16[1024,2048]{1,0:T(8,128)(2,1)} async-done(((bf16[64,2048]{1,0:T(8,128)(2,1)}), bf16[1024,2048]{1,0:T(8,128)(2,1)}) %all-gather.2.cloned.1.call-update) | async-done | bytes 4194320 | tf_op jit(solution)/shard_map/all_gather | solution.py:15
  118.6 2.1 convert_reduce_fusion
  120.6 2.3 fusion.4
  122.9 0.0 copy-done.8
  123.0 0.0 copy-done
  123.0 0.0 copy-start.6
  123.0 1.3 convolution_convert_fusion.2
  124.3 0.2 copy.17
  124.5 0.9 gather_fusion
  125.3 0.1 broadcast_select_fusion
  125.4 2.8 %collective-permute-start.1 = (bf16[256,128]{1,0:T(8,128)(2,1)S(1)}, bf16[256,128]{1,0:T(8,128)(2,1)S(1)}, u32[]{:S(2)}, u32[]{:S(2)}) collective-permute-start(bf16[256,128]{1,0:T(8,128)(2,1)S(1)} %broadcast_select_fusion), channel_id=1, source_target_pairs={{0,1},{1,2},{2,3},{3,4},{4,5},{5,6},{6,7},{7,8},{8,9},{9,10},{10,1... | collective-permute-start | bytes 196616 | tf_op jit(solution)/shard_map/ppermute | solution.py:36
  128.2 0.0 copy-done.6
  128.3 3.1 %fusion.16 = f32[1024,64]{0,1:T(8,128)} fusion(bf16[1024,2048]{1,0:T(8,128)(2,1)} %all-gather.2.cloned.1.call-done, f32[1024]{0:T(1024)S(1)} %copy-done.6, bf16[1024,256]{1,0:T(8,128)(2,1)S(1)} %all_gather.7), kind=kOutput, calls=%fused_computation.22 | convolution fusion | flops 137363456 | bytes 2625536 | tf_op jit(solution)/shard_map/dot_general | solution.py:88
  131.4 0.7 slice.28
  132.1 0.7 copy.63
  132.8 0.0 collective-permute-done.1
  132.8 0.1 copy.19
  132.9 1.5 fusion.54
  134.5 0.0 copy-done.2
  134.5 4.0 %fusion.89 = (f32[2,512]{1,0:T(2,128)}, f32[2,512,640]{2,1,0:T(8,128)}) fusion(pred[2,640]{1,0:T(4,128)(4,1)} %concatenate.20, bf16[8,2,8,512]{3,2,1,0:T(8,128)(2,1)} %bitcast.62, bf16[2,512,128]{1,2,0:T(8,128)(2,1)S(1)} %bitcast.58, bf16[2,128,128]{1,2,0:T(8,128)(2,1)S(1)} %copy.19), kind=kOutput, calls=%fused_computation.94 | convolution fusion | flops 86835840 | bytes 3085568 | tf_op jit(solution)/shard_map/sub | solution.py:80
  138.5 2.3 fusion.29
  140.8 3.1 %fusion.27 = bf16[2,8,8,512]{3,2,1,0:T(8,128)(2,1)} fusion(f32[2,512]{1,0:T(2,128)S(1)} %get-tuple-element.6, bf16[2,128,128]{1,2,0:T(8,128)(2,1)S(1)} %copy.19, bf16[2,512,128]{1,2,0:T(8,128)(2,1)} %bitcast.56, f32[2,512]{1,0:T(2,128)} %get-tuple-element.7, pred[2,640]{1,0:T(4,128)(4,1)} %concatenate.20, bf16[8,2,8,512]{3,2,1,0:T(8,128)(2,1)} %bitcast.64), kind=kOutput, calls=%fused_computation.35 | convolution fusion | flops 171837056 | bytes 928256 | tf_op jit(solution)/shard_map/wqk,wkd->wqd/dot_general | solution.py:84
  143.9 8.7 %fusion.23 = bf16[2,512,64]{1,2,0:T(8,128)(2,1)} fusion(f32[2,512,640]{2,1,0:T(8,128)S(1)} %fusion.54, bf16[2,512,128]{1,2,0:T(8,128)(2,1)} %bitcast.57, bf16[2,128,128]{1,2,0:T(8,128)(2,1)S(1)} %copy.19, f32[2,512,640]{2,1,0:T(8,128)} %get-tuple-element.8, f32[2,512]{1,0:T(2,128)} %get-tuple-element.7), kind=kOutput, calls=%fused_computation.33 | convolution fusion | flops 88868480 | bytes 10952704 | tf_op jit(solution)/shard_map/wqk,wkd->wqd/dot_general | solution.py:98
  152.5 8.9 %fusion.10 = f32[2,640,64]{1,2,0:T(8,128)} fusion(f32[2,512,640]{2,1,0:T(8,128)S(1)} %fusion.54, bf16[8,2,8,512]{3,2,1,0:T(8,128)(2,1)} %bitcast.65, f32[2,512,640]{2,1,0:T(8,128)} %get-tuple-element.8, f32[2,512]{1,0:T(2,128)} %get-tuple-element.7), kind=kOutput, calls=%fused_computation.18 | convolution fusion | flops 88475264 | bytes 5705728 | tf_op jit(solution)/shard_map/wqk,wqd->wkd/dot_general | solution.py:101
  161.4 1.0 copy.35
  162.4 0.9 fusion.46
  163.2 0.1 copy.25
  163.4 2.1 collective-permute-start.2
  165.5 2.2 fusion.22
  167.7 0.0 copy-start.9
  167.7 0.1 fusion.31
  167.7 0.2 copy.24
  167.9 0.2 copy.29
  168.1 0.9 reshape.141
  169.0 11.3 %all-to-all-start.2 = ((bf16[32,2,1024]{2,1,0:T(2,128)(2,1)}), bf16[32,2,1024]{2,1,0:T(2,128)(2,1)S(1)}, u32[]{:S(2)}, u32[]{:S(2)}) async-start(bf16[32,2,1024]{2,1,0:T(2,128)(2,1)} %reshape.141), calls=%async_computation.2 | async-start | bytes 262144 | tf_op jit(solution)/shard_map/all_to_all | solution.py:46
  180.3 0.2 copy.30
  180.4 0.0 collective-permute-done.2
  180.5 2.3 scatter_custom_fusion
  182.8 2.9 %convolution_convert_fusion.1 = bf16[1024,192]{0,1:T(8,128)(2,1)S(1)} fusion(f32[1024]{0:T(1024)S(1)} %copy-done.9, f32[1024]{0:T(1024)S(1)} %broadcast_add_fusion, bf16[1024,128]{1,0:T(8,128)(2,1)S(1)} %convert.12, bf16[1024,64]{1,0:T(8,128)(2,1)S(1)} %bitcast.52, f32[1024]{0:T(1024)S(1)} %add_rsqrt_fusion, f32[1024]{0:T(1024)S(1)} %broadcast_multiply_fusion, ...), kind=kOutput, calls=%fused_computation.29 | convolution fusion | flops 409927680 | bytes 2899968 | tf_op jit(solution)/shard_map/dot_general | solution.py:135
  185.7 1.0 copy.27
  186.7 4.1 %all-to-all-done.2 = bf16[32,2,1024]{2,1,0:T(2,128)(2,1)S(1)} async-done(((bf16[32,2,1024]{2,1,0:T(2,128)(2,1)}), bf16[32,2,1024]{2,1,0:T(2,128)(2,1)S(1)}, u32[]{:S(2)}, u32[]{:S(2)}) %all-to-all-start.2) | async-done | bytes 131104 | tf_op jit(solution)/shard_map/all_to_all | solution.py:46
  190.8 5.8 %all-to-all-start.1 = ((bf16[32,32,192]{2,1,0:T(8,128)(2,1)}), bf16[32,32,192]{2,1,0:T(8,128)(2,1)S(1)}, u32[]{:S(2)}, u32[]{:S(2)}) async-start(bf16[32,32,192]{2,1,0:T(8,128)(2,1)} %bitcast.7), calls=%async_computation.1 | async-start | bytes 1048576 | tf_op jit(solution)/shard_map/all_to_all | solution.py:46
  196.5 2.2 convolution_convert_fusion
  198.7 15.9 %all-to-all-done.1 = bf16[32,32,192]{2,1,0:T(8,128)(2,1)S(1)} async-done(((bf16[32,32,192]{2,1,0:T(8,128)(2,1)}), bf16[32,32,192]{2,1,0:T(8,128)(2,1)S(1)}, u32[]{:S(2)}, u32[]{:S(2)}) %all-to-all-start.1) | async-done | bytes 393248 | tf_op jit(solution)/shard_map/all_to_all | solution.py:46
  214.6 6.3 %all-to-all-start = ((bf16[16,64,1024]{2,1,0:T(8,128)(2,1)}), bf16[16,64,1024]{2,1,0:T(8,128)(2,1)S(1)}, u32[]{:S(2)}, u32[]{:S(2)}) async-start(bf16[16,64,1024]{2,1,0:T(8,128)(2,1)} %bitcast.6), calls=%async_computation | async-start | bytes 4194304 | tf_op jit(solution)/shard_map/all_to_all | solution.py:46
  221.0 0.1 dynamic-slice.3
  221.0 4.1 %fusion.2 = f32[1024,1024]{1,0:T(8,128)} fusion(f32[1024]{0:T(1024)S(1)} %add_rsqrt_fusion, f32[1024]{0:T(1024)S(1)} %broadcast_multiply_fusion, bf16[1024,2048]{1,0:T(8,128)(2,1)} %all-gather.2.cloned.1.call-done), kind=kLoop, calls=%fused_computation.6 | loop fusion | flops 3145728 | bytes 6299648 | tf_op jit(solution)/shard_map/mul | solution.py:56
  225.1 0.2 reshape.142
  225.3 0.7 convert_reduce_fusion.3
  226.0 0.7 convert_reduce_fusion.2
  226.7 42.7 %all-to-all-done = bf16[16,64,1024]{2,1,0:T(8,128)(2,1)S(1)} async-done(((bf16[16,64,1024]{2,1,0:T(8,128)(2,1)}), bf16[16,64,1024]{2,1,0:T(8,128)(2,1)S(1)}, u32[]{:S(2)}, u32[]{:S(2)}) %all-to-all-start) | async-done | bytes 2097184 | tf_op jit(solution)/shard_map/all_to_all | solution.py:46
  269.4 0.4 convert_reduce_fusion.1
  269.7 1.1 multiply_reduce_fusion.2
  270.9 1.7 add_convert_fusion.3
  (22 shorter events, 0.1 us)
Async XLA Ops:
  7.2 111.4 %all-gather.2.cloned.1.call-start = ((), (), s32[]{:S(2)}) async-start(), calls=%async_computation.3 | async-start | bytes 4456448 | tf_op jit(solution)/shard_map/all_gather | solution.py:15
  8.9 114.1 %copy-start.8 = (f32[1024]{0:T(1024)S(1)}, f32[1024]{0:T(1024)}, u32[]{:S(2)}) copy-start(f32[1024]{0:T(1024)} %param.14) | copy-start | bytes 12292
  8.9 56.1 %collective-permute-start = (s32[256]{0:T(256)}, s32[256]{0:T(256)S(1)}, u32[]{:S(2)}, u32[]{:S(2)}) collective-permute-start(s32[256]{0:T(256)} %bitcast.70), channel_id=1, source_target_pairs={{1,0},{2,1},{3,2},{4,3},{5,4},{6,5},{7,6},{8,7},{9,8},{10,9},{11,1... | collective-permute-start | bytes 3080 | tf_op jit(solution)/shard_map/ppermute | solution.py:36
  65.0 53.5 %copy-start.5 = (s32[256]{0:T(256)}, s32[256]{0:T(256)S(1)}, u32[]{:S(2)}) copy-start(s32[256]{0:T(256)S(1)} %compare_select_fusion) | copy-start | bytes 3076
  118.6 4.4 %copy-start = (bf16[1024,2048]{1,0:T(8,128)(2,1)S(1)}, bf16[1024,2048]{1,0:T(8,128)(2,1)}, u32[]{:S(2)}) copy-start(bf16[1024,2048]{1,0:T(8,128)(2,1)} %all-gather.2.cloned.1.call-done) | copy-start | bytes 12582916
  123.0 5.3 %copy-start.6 = (f32[1024]{0:T(1024)S(1)}, f32[1024]{0:T(1024)}, u32[]{:S(2)}) copy-start(f32[1024]{0:T(1024)} %param.15) | copy-start | bytes 12292
  125.4 7.4 %collective-permute-start.1 = (bf16[256,128]{1,0:T(8,128)(2,1)S(1)}, bf16[256,128]{1,0:T(8,128)(2,1)S(1)}, u32[]{:S(2)}, u32[]{:S(2)}) collective-permute-start(bf16[256,128]{1,0:T(8,128)(2,1)S(1)} %broadcast_select_fusion), channel_id=1, source_target_pairs={{0,1},{1,2},{2,3},{3,4},{4,5},{5,6},{6,7},{7,8},{8,9},{9,10},{10,1... | collective-permute-start | bytes 196616 | tf_op jit(solution)/shard_map/ppermute | solution.py:36
  132.8 1.7 copy-start.2
  152.5 12.9 %copy-start.7 = (f32[1024]{0:T(1024)S(1)}, f32[1024]{0:T(1024)}, u32[]{:S(2)}) copy-start(f32[1024]{0:T(1024)} %param.15) | copy-start | bytes 12292
  161.4 6.3 %copy-start.1 = (f32[2,640,64]{1,2,0:T(8,128)S(1)}, f32[2,640,64]{1,2,0:T(8,128)}, u32[]{:S(2)}) copy-start(f32[2,640,64]{1,2,0:T(8,128)} %fusion.10) | copy-start | bytes 983044
  163.4 17.1 %collective-permute-start.2 = (bf16[256,128]{1,0:T(8,128)(2,1)S(1)}, bf16[256,128]{1,0:T(8,128)(2,1)S(1)}, u32[]{:S(2)}, u32[]{:S(2)}) collective-permute-start(bf16[256,128]{1,0:T(8,128)(2,1)S(1)} %bitcast.67), channel_id=1, source_target_pairs={{1,0},{2,1},{3,2},{4,3},{5,4},{6,5},{7,6},{8,7},{9,8},{10,9},{11,1... | collective-permute-start | bytes 196616 | tf_op jit(solution)/shard_map/ppermute | solution.py:36
  165.5 14.8 %copy-start.4 = (bf16[2,512,64]{1,2,0:T(8,128)(2,1)S(1)}, bf16[2,512,64]{1,2,0:T(8,128)(2,1)}, u32[]{:S(2)}) copy-start(bf16[2,512,64]{1,2,0:T(8,128)(2,1)} %fusion.23) | copy-start | bytes 393220
  167.7 15.1 %copy-start.9 = (f32[1024]{0:T(1024)S(1)}, f32[1024]{0:T(1024)}, u32[]{:S(2)}) copy-start(f32[1024]{0:T(1024)} %param.14) | copy-start | bytes 12292
  169.0 21.8 %all-to-all-start.2 = ((bf16[32,2,1024]{2,1,0:T(2,128)(2,1)}), bf16[32,2,1024]{2,1,0:T(2,128)(2,1)S(1)}, u32[]{:S(2)}, u32[]{:S(2)}) async-start(bf16[32,2,1024]{2,1,0:T(2,128)(2,1)} %reshape.141), calls=%async_computation.2 | async-start | bytes 262144 | tf_op jit(solution)/shard_map/all_to_all | solution.py:46
  190.8 23.9 %all-to-all-start.1 = ((bf16[32,32,192]{2,1,0:T(8,128)(2,1)}), bf16[32,32,192]{2,1,0:T(8,128)(2,1)S(1)}, u32[]{:S(2)}, u32[]{:S(2)}) async-start(bf16[32,32,192]{2,1,0:T(8,128)(2,1)} %bitcast.7), calls=%async_computation.1 | async-start | bytes 1048576 | tf_op jit(solution)/shard_map/all_to_all | solution.py:46
  214.6 54.7 %all-to-all-start = ((bf16[16,64,1024]{2,1,0:T(8,128)(2,1)}), bf16[16,64,1024]{2,1,0:T(8,128)(2,1)S(1)}, u32[]{:S(2)}, u32[]{:S(2)}) async-start(bf16[16,64,1024]{2,1,0:T(8,128)(2,1)} %bitcast.6), calls=%async_computation | async-start | bytes 4194304 | tf_op jit(solution)/shard_map/all_to_all | solution.py:46
  225.1 45.8 %copy-start.3 = (bf16[64,1024]{1,0:T(8,128)(2,1)S(1)}, bf16[64,1024]{1,0:T(8,128)(2,1)}, u32[]{:S(2)}) copy-start(bf16[64,1024]{1,0:T(8,128)(2,1)} %param.10) | copy-start | bytes 393220
Sparse Core Ops, SparseCore 0:
  10.1 108.4 all-gather.1
where the time goes:
time: 281 us; the launch traced here: 279 us
  waiting for transfers between devices  116 us (41%)
  blocking collectives  44.5 us (16%)
  matrix products  40.1 us (14%)
  starting transfers between devices  37.1 us (13%)
  other arithmetic  20.3 us (7%)
  between operations  14.4 us (5%)
  local copies, waits for them, and re-layouts  6.96 us (2%)
    all_to_all x3, waiting for transfers between devices, sum_at_owner(): lax.all_to_all(blocks, axis, split_axis=0, concat_axis=0, tiled=True)  62.6 us
    all_gather x1, waiting for transfers between devices, in_one_piece(): whole = lax.all_gather(both, axis, axis=dim, tiled=True)  53.5 us
    all_gather x1, blocking collectives, turned_gather(): whole = lax.all_gather(both, axis, axis=0, tiled=True)  44.5 us
    all_to_all x3, starting transfers between devices, sum_at_owner(): lax.all_to_all(blocks, axis, split_axis=0, concat_axis=0, tiled=True)  23.4 us
    ppermute x3, starting transfers between devices, shifted(): return lax.ppermute(block, axis, route)  13.7 us
    dot_general x1, matrix products, attend(): jnp.einsum('wqk,wqd->wkd', grad_score, query_win, preferred_element_type=...  8.88 us
    dot_general x1, matrix products, attend(): jnp.einsum('wqk,wkd->wqd', grad_score, key_part, preferred_element_type=j...  8.65 us
  transfers between devices with their start and end apart: 7, of which 4 were waited for; matrix products, arithmetic and copies ran while one was open for 9% of the time, Pallas kernels for 0%

commit v1 on v0

v1 whole, which is shorter than its diff:
```python
import functools

import jax
import jax.numpy as jnp
from jax import lax
from jax.experimental import pallas as pl
from jax.experimental.pallas import tpu as pltpu
from jax.sharding import PartitionSpec as P

HD = 64
EPS = 1e-06
NEG = -1000000000.0
MESH = pl.DeviceIdType.MESH
F32 = jnp.float32
BF16 = jnp.bfloat16


def dot(a, b, dims=((1,), (0,))):
    return lax.dot_general(a, b, (dims, ((), ())), preferred_element_type=F32)


def kernel(
    ny, nxh, nz, win, edge,
    tok, cot, wq, wo, scale, shift, gate, counts, edges,
    out_tok, out_w,
    nrm, nx, inv, act, xt, wbuf, meta_nat, meta_own, meta_next,
    kv, kvt, qa, oh, e_send, e_recv, g_send, g_recv, gkv, gg,
    pv_send, pv_recv, dwf, dwb, r1, s2, r2, s3, r3,
    f1s, f1r, f2s, f2r, wzs, wzr, wxs, wxr, wcs, wcr,
    ms, mr, es, er, gs, gr, dcs, dcr, dxs, dxr, dzs, dzr, ps, pr,
):
    ns = nxh * nz * 2
    nyh = ny // 2
    nxx = 2 * nxh
    own = tok.shape[0]
    blk = 2 * own
    d_model = tok.shape[1]
    wr = wq.shape[0]

    enc = lax.axis_index("enc")
    slab = lax.axis_index("slab")
    y, xl = enc // 2, enc % 2
    xh, z, c = slab // (2 * nz), (slab // 2) % nz, slab % 2
    x = xh * 2 + xl
    mine = xh * 2 * nz + z * 2 + xl
    after = (mine + 1) % ns
    before = (mine + ns - 1) % ns
    half = y // nyh

    def at(y_, xl_, xh_, z_, c_):
        return {"enc": y_ * 2 + xl_, "slab": xh_ * (2 * nz) + z_ * 2 + c_}

    def at_slab(s_, c_):
        return {"enc": y * 2 + s_ % 2, "slab": (s_ // 2) * 2 + c_}

    sibling = at(y, xl, xh, z, 1 - c)
    up = at((y + 1) % ny, xl, xh, z, c)
    down = at((y + ny - 1) % ny, xl, xh, z, c)

    def z_peer(j):
        return at(y, xl, xh, (z + j) % nz, c)

    def x_peer(j):
        xx = (x + j) % nxx
        return at(y, xx % 2, xx // 2, z, c)

    def copy(src, dst, send, recv, to):
        return pltpu.make_async_remote_copy(
            src_ref=src, dst_ref=dst, send_sem=send, recv_sem=recv, device_id=to, device_id_type=MESH
        )

    at_home = jnp.logical_and(c == xl, half == c)
    away = jnp.logical_not(at_home)
    diag = c == xl

    barrier = pltpu.get_barrier_semaphore()

    def greet(to):
        pl.semaphore_signal(barrier, inc=1, device_id=to, device_id_type=MESH)

    greet(sibling)
    greet(up)
    greet(down)
    for j in range(1, nz):
        greet(z_peer(j))
    for j in range(1, nxx):
        greet(x_peer(j))
    for k in range(2):
        greet(at_slab(after, k))
        greet(at_slab(before, k))

    @pl.when(half == c)
    def _():
        greet(at(y, 1 - xl, xh, z, xl))

    @pl.when(jnp.logical_and(half == c, xl != c))
    def _():
        greet(at(y, xl, xh, z, xl))

    for yy in range(ny):

        @pl.when(jnp.logical_or(away, yy != y))
        def _():
            greet(at(yy, c, xh, z, half))

    greeted = 3 + (nz - 1) + (nxx - 1) + 4 + (ny + 1) - 2 * at_home.astype(jnp.int32)

    widened = tok[...].astype(F32)
    average = jnp.mean(widened, 1, keepdims=True)
    centred = widened - average
    variance = jnp.mean(centred * centred, 1, keepdims=True)
    inv_std = lax.rsqrt(variance + EPS)
    normal = centred * inv_std
    gain = 1.0 + scale[...]
    nx[...] = normal
    inv[...] = jnp.broadcast_to(inv_std, inv.shape)
    nrm[0] = (normal * gain + shift[...]).astype(BF16)
    nrm[1] = (cot[...].astype(F32) * gate[...]).astype(BF16)

    hd = wo.shape[0]
    eye = (
        lax.broadcasted_iota(jnp.int32, (wr, wr), 0) == lax.broadcasted_iota(jnp.int32, (wr, wr), 1)
    ).astype(F32).astype(BF16)
    wo_t = dot(eye, wo[...], ((1,), (1,))).astype(BF16)
    wq_here = wq[...]
    wbuf[xl, xh, z, c] = jnp.concatenate([wq_here[:, hd : 3 * hd], wq_here[:, :hd], wo_t], 1)

    meta_nat[...] = jnp.zeros(meta_nat.shape, jnp.int32)
    meta_nat[0:2, :] = edges[...]
    meta_nat[2:3, :] = jnp.full((1, edge), counts[0], jnp.int32)
    meta_nat[3:4, :] = jnp.full((1, edge), counts[1], jnp.int32)

    @pl.when(diag)
    def _():
        meta_own[...] = meta_nat[...]

    r_own = (y % nyh) * blk + xl * own
    home = at(y, c, xh, z, half)

    @pl.when(at_home)
    def _():
        for p in range(2):
            act[p, pl.ds(pl.multiple_of(r_own, own), own), :] = nrm[p]

    pl.semaphore_wait(barrier, greeted)

    def f1(p):
        return copy(
            nrm.at[p],
            act.at[p, pl.ds(pl.multiple_of(r_own, own), own)],
            f1s.at[p],
            f1r.at[xl, p],
            home,
        )

    for p in range(2):

        @pl.when(away)
        def _():
            f1(p).start()

    def wz(j):
        return copy(wbuf.at[xl, xh, z, c], wbuf.at[xl, xh, z, c], wzs.at[j], wzr.at[j], z_peer(j))

    def wz_in(j):
        block = wbuf.at[xl, xh, (z + nz - j) % nz, c]
        return copy(block, block, wzs.at[j], wzr.at[j], z_peer(j))

    for j in range(1, nz):
        wz(j).start()

    def meta_out(n):
        if n == 0:
            return copy(meta_nat, meta_own, ms.at[0], mr.at[0], sibling)
        return copy(meta_nat, meta_next, ms.at[n], mr.at[1], at_slab(before, n - 1))

    @pl.when(diag)
    def _():
        for n in range(3):
            meta_out(n).start()

    def f1_in(h, p):
        rows = pl.ds(pl.multiple_of((y % nyh) * blk + h * own, own), own)
        return copy(nrm.at[p], act.at[p, rows], f1s.at[p], f1r.at[h, p], sibling)

    def ring(i, p, way):
        rows = pl.ds(pl.multiple_of(i * blk, blk), blk)
        return copy(
            act.at[p, rows], act.at[p, rows], f2s.at[i, p, way], f2r.at[i, p], up if way == 0 else down
        )

    here = y % nyh

    for p in range(2):
        for h in range(2):

            @pl.when(jnp.logical_and(half == c, jnp.logical_or(away, h != xl)))
            def _():
                f1_in(h, p).wait_recv()

        @pl.when(half == c)
        def _():
            ring(here, p, p).start()

    if nyh > 1:

        @pl.when(half == c)
        def _():
            ring(here, 1, 0).start()
            ring(here, 0, 1).start()

    def turn(i):
        rows = pl.ds(pl.multiple_of(i * blk, blk), blk)
        for p in range(2):
            cols = pl.ds(pl.multiple_of(p * win + i * blk, blk), blk)
            xt[:, cols] = act[p, rows, :].T

    def project(i):
        rows = pl.ds(pl.multiple_of(i * blk, blk), blk)
        lane = lax.broadcasted_iota(jnp.int32, (blk, 2 * HD), 1)
        row = lax.broadcasted_iota(jnp.int32, (blk, 2 * HD), 0) + i * blk
        live = row < jnp.where(c == 0, meta_own[2:3, :], meta_own[3:4, :])
        for h in range(2):
            w = wbuf[h].reshape(d_model, 4 * HD)
            from_normed = dot(act[0, rows, :], w)
            from_upstream = dot(act[1, rows, :], w[:, 2 * HD :])
            kv[h, rows, :] = from_normed[:, : 2 * HD].astype(BF16)
            query = from_normed[:, 2 * HD :].astype(BF16).astype(F32) * (HD**-0.5)
            qa[h, 0, rows, :] = jnp.where(lane < HD, query, 0.0).astype(BF16)
            qa[h, 1, rows, :] = jnp.where(
                jnp.logical_and(lane >= HD, live), from_upstream, 0.0
            ).astype(BF16)

    @pl.when(half == c)
    def _():
        turn(here)

    def wx(j):
        block = wbuf.at[xl, xh, :, c]
        return copy(block, block, wxs.at[j], wxr.at[j], x_peer(j))

    def wx_in(j):
        xx = (x + nxx - j) % nxx
        block = wbuf.at[xx % 2, xx // 2, :, c]
        return copy(block, block, wxs.at[j], wxr.at[j], x_peer(j))

    def wc(k):
        block = wbuf.at[:, :, :, k]
        return copy(block, block, wcs, wcr, sibling)

    def weights_x():
        for j in range(1, nz):
            wz_in(j).wait_recv()
        for j in range(1, nxx):
            wx(j).start()

    def weights_core():
        for j in range(1, nxx):
            wx_in(j).wait_recv()
        wc(c).start()

    def weights_done():
        wc(1 - c).wait_recv()

        @pl.when(jnp.logical_not(diag))
        def _():
            meta_out(0).wait_recv()

        meta_out(1).wait_recv()

    def far(i):
        return (y + ny - i - nyh * c) % ny == nyh

    stages = [weights_x, weights_core, weights_done]
    for t in range(1, nyh + 1):
        if t == nyh:
            for stage in stages:
                stage()
            stages = []

            @pl.loop(0, nyh)
            def _(i):
                @pl.when(jnp.logical_not(far(i)))
                def _():
                    project(i)

        elif stages:
            stages.pop(0)()
        from_below = (y + 2 * ny - t - nyh * c) % ny
        from_above = (y + 2 * ny + t - nyh * c) % ny
        has_below = from_below < nyh
        has_above = from_above < nyh

        @pl.when(has_below)
        def _():
            ring(from_below, 0, 0).wait_recv()
            if t < nyh:
                ring(from_below, 0, 0).start()

        @pl.when(has_above)
        def _():
            ring(from_above, 1, 1).wait_recv()
            if t < nyh:
                ring(from_above, 1, 1).start()

        if t < nyh:

            @pl.when(has_below)
            def _():
                ring(from_below, 1, 0).wait_recv()
                if t < nyh - 1:
                    ring(from_below, 1, 0).start()

            @pl.when(has_above)
            def _():
                ring(from_above, 0, 1).wait_recv()
                if t < nyh - 1:
                    ring(from_above, 0, 1).start()

            @pl.when(has_above)
            def _():
                turn(from_above)

        @pl.when(has_below)
        def _():
            turn(from_below)
            if t == nyh:
                project(from_below)

    row_id = lax.broadcasted_iota(jnp.int32, (win, edge), 0) + c * win
    for k in range(2):
        oh[:, k * edge : (k + 1) * edge] = (row_id == meta_next[k : k + 1, :]).astype(F32).astype(BF16)
    for h in range(2):
        kvt[h, :, :win] = kv[h, :win, :].T
    for h in range(2):
        picked = dot(kvt[h, :, :win], oh[...]).astype(BF16)
        for k in range(2):
            e_send[k, h] = picked[:, k * edge : (k + 1) * edge]

    def edge_out(k):
        return copy(e_send.at[k], e_recv.at[c], es.at[k], er.at[c], at_slab(after, k))

    def edge_in(k):
        return copy(e_send.at[k], e_recv.at[k], es.at[k], er.at[k], sibling)

    for k in range(2):
        edge_out(k).start()
    for k in range(2):
        edge_in(k).wait_recv()
    for h in range(2):
        arrived = e_recv[0, h].astype(F32) + e_recv[1, h].astype(F32)
        kvt[h, :, win:] = arrived.astype(BF16)
        kv[h, win:, :] = arrived.T.astype(BF16)

    keys = win + edge
    step = 256 if win % 256 == 0 else win
    has_edge = mine > 0
    count = jnp.where(c == 0, meta_own[2:3, :], meta_own[3:4, :])
    limit = jnp.concatenate([count] * (step // edge), 1)

    def attend(h):
        gkv[h] = jnp.zeros(gkv.shape[1:], F32)

        @pl.loop(0, win // step)
        def _(n):
            q_rows = pl.ds(pl.multiple_of(n * step, step), step)
            query = qa[h, 0, q_rows, :]
            g_att = qa[h, 1, q_rows, :]
            key_id = lax.broadcasted_iota(jnp.int32, (keys, step), 0)
            key_live = jnp.logical_or(
                key_id < limit, jnp.logical_and(key_id >= win, has_edge)
            )
            scores = jnp.where(key_live, dot(kv[h], query, ((1,), (1,))), NEG)
            exponent = jnp.exp(scores - jnp.max(scores, 0, keepdims=True))
            probs = exponent * (1.0 / jnp.sum(exponent, 0, keepdims=True))
            weights = probs.astype(BF16)
            g_prob = dot(kv[h], g_att, ((1,), (1,)))
            centre = jnp.sum(g_prob * probs, 0, keepdims=True)
            g_score = (probs * (g_prob - centre)).astype(BF16)
            lane = lax.broadcasted_iota(jnp.int32, (HD, step), 1) + n * step
            attended = jnp.where(lane < limit, dot(kvt[h, HD:, :], weights), 0.0)
            g_query = dot(kvt[h, :HD, :], g_score) * (HD**-0.5)
            pair = jnp.concatenate([g_query, attended], 0).T
            side = lax.broadcasted_iota(jnp.int32, (step, 2 * HD), 1)
            gg[h, q_rows, 2 * HD :] = jnp.where(side < HD, pair, 0.0).astype(BF16)
            low = pl.ds(pl.multiple_of(win + n * step, step), step)
            gg[h, low, 2 * HD :] = jnp.where(side >= HD, pair, 0.0).astype(BF16)
            gg[h, low, : 2 * HD] = jnp.zeros((step, 2 * HD), BF16)
            gkv[h] += dot(g_score, query) + dot(weights, g_att)

        g_send[h] = gkv[h, win:, :].astype(BF16)

    def grad_out(h, k):
        return copy(g_send.at[h], g_recv.at[h, c], gs.at[h, k], gr.at[h, c], at_slab(before, k))

    def grad_in(h, k):
        return copy(g_send.at[h], g_recv.at[h, k], gs.at[h, k], gr.at[h, k], sibling)

    for h in range(2):
        attend(h)
        for k in range(2):
            grad_out(h, k).start()
    for h in range(2):
        for k in range(2):
            grad_in(h, k).wait_recv()
        returned = dot(oh[...], g_recv[h].reshape(2 * edge, 2 * HD))
        gg[h, :win, : 2 * HD] = (gkv[h, :win, :] + returned).astype(BF16)

    def part_out(j):
        yy = nyh * c + j // 2
        return copy(pv_send.at[j], pv_recv.at[y], ps.at[j], pr.at[y], at(yy, j % 2, xh, z, xl))

    def part_in(yy):
        return copy(pv_send.at[0], pv_recv.at[yy], ps.at[0], pr.at[yy], sibling)

    def is_mine(j):
        return jnp.logical_and(at_home, enc == 2 * nyh * c + j)

    for b in range(nyh):
        rows = pl.ds(b * blk, blk)
        total = jnp.zeros((blk, d_model), F32)
        for h in range(2):
            total += dot(gg[h, rows, :], wbuf[h].reshape(d_model, 4 * HD), ((1,), (1,)))
        value = total.astype(BF16)
        for k in range(2):
            j = 2 * b + k
            pv_send[j] = value[k * own : (k + 1) * own, :]

            @pl.when(jnp.logical_not(is_mine(j)))
            def _():
                part_out(j).start()

            @pl.when(is_mine(j))
            def _():
                pv_recv[y] = pv_send[j]

    for h in range(2):
        grad_w = dot(xt[...], gg[h]).reshape(nxh, nz, 2, wr, 4 * HD)
        dwf[h] = grad_w
        dwb[h] = grad_w.astype(BF16)

    def dc(k):
        return copy(dwb.at[:, :, :, k], r1, dcs, dcr, sibling)

    dc(1 - c).start()
    dc(1 - c).wait_recv()
    for h in range(2):
        s2[h] = (dwf[h, :, :, c] + r1[h].astype(F32)).astype(BF16)

    def dx(j):
        xx = (x + j) % nxx
        return copy(s2.at[xx % 2, xx // 2], r2.at[j], dxs.at[j], dxr.at[j], x_peer(j))

    for j in range(1, nxx):
        dx(j).start()
    total = dwf[xl, xh, :, c] + r1[xl, xh].astype(F32)
    for j in range(1, nxx):
        dx(j).wait_recv()
        total += r2[j].astype(F32)
    dwf[0, 0, :, 0] = total
    s3[...] = total.astype(BF16)

    def dz(j):
        return copy(s3.at[(z + j) % nz], r3.at[j], dzs.at[j], dzr.at[j], z_peer(j))

    for j in range(1, nz):
        dz(j).start()
    final = dwf[0, 0, z, 0]
    for j in range(1, nz):
        dz(j).wait_recv()
        final += r3[j].astype(F32)
    out_w[...] = final

    mine_sum = jnp.zeros((own, d_model), F32)
    for yy in range(ny):

        @pl.when(jnp.logical_or(away, yy != y))
        def _():
            part_in(yy).wait_recv()

    for yy in range(ny):
        mine_sum += pv_recv[yy].astype(F32)
    g_hat = mine_sum * gain
    normal_own = nx[...]
    g_tok = cot[...].astype(F32) + inv[:, 0:1] * (
        g_hat
        - jnp.mean(g_hat, 1, keepdims=True)
        - normal_own * jnp.mean(g_hat * normal_own, 1, keepdims=True)
    )
    out_tok[...] = g_tok.astype(BF16)

    for p in range(2):

        @pl.when(away)
        def _():
            f1(p).wait_send()

    for j in range(1, nz):
        wz(j).wait_send()
        dz(j).wait_send()
    for j in range(1, nxx):
        wx(j).wait_send()
        dx(j).wait_send()
    wc(c).wait_send()
    dc(1 - c).wait_send()

    @pl.when(diag)
    def _():
        for n in range(3):
            meta_out(n).wait_send()

    for i in range(nyh):
        apart = (y + ny - i - nyh * c) % ny

        @pl.when(apart < nyh)
        def _():
            ring(i, 0, 0).wait_send()

        @pl.when(apart < nyh - 1)
        def _():
            ring(i, 1, 0).wait_send()

        back = (ny - apart) % ny

        @pl.when(back < nyh)
        def _():
            ring(i, 1, 1).wait_send()

        @pl.when(back < nyh - 1)
        def _():
            ring(i, 0, 1).wait_send()

    for k in range(2):
        edge_out(k).wait_send()
        for h in range(2):
            grad_out(h, k).wait_send()
    for j in range(2 * nyh):

        @pl.when(jnp.logical_not(is_mine(j)))
        def _():
            part_out(j).wait_send()


def on_device(nxh, tokens, cotangent, w_qkv, w_out, mod_scale, mod_shift, mod_gate, counts, edge_index):
    ny = lax.axis_size("enc") // 2
    nz = lax.axis_size("slab") // (2 * nxh)
    own, d_model = tokens.shape
    edge = edge_index.shape[1]
    win = own * ny
    wr = w_qkv.shape[0]
    nyh, nxx = ny // 2, 2 * nxh
    wide = 4 * HD
    dma = pltpu.SemaphoreType.DMA
    vmem = pl.BlockSpec(memory_space=pltpu.VMEM)
    scratch = [
        pltpu.VMEM((2, own, d_model), BF16),
        pltpu.VMEM((own, d_model), F32),
        pltpu.VMEM((own, 128), F32),
        pltpu.VMEM((2, win, d_model), BF16),
        pltpu.VMEM((d_model, 2 * win), BF16),
        pltpu.VMEM((2, nxh, nz, 2, wr, wide), BF16),
        pltpu.VMEM((8, edge), jnp.int32),
        pltpu.VMEM((8, edge), jnp.int32),
        pltpu.VMEM((8, edge), jnp.int32),
        pltpu.VMEM((2, win + edge, 2 * HD), BF16),
        pltpu.VMEM((2, 2 * HD, win + edge), BF16),
        pltpu.VMEM((2, 2, win, 2 * HD), BF16),
        pltpu.VMEM((win, 2 * edge), BF16),
        pltpu.VMEM((2, 2, 2 * HD, edge), BF16),
        pltpu.VMEM((2, 2, 2 * HD, edge), BF16),
        pltpu.VMEM((2, edge, 2 * HD), BF16),
        pltpu.VMEM((2, 2, edge, 2 * HD), BF16),
        pltpu.VMEM((2, win + edge, 2 * HD), F32),
        pltpu.VMEM((2, 2 * win, wide), BF16),
        pltpu.VMEM((2 * nyh, own, d_model), BF16),
        pltpu.VMEM((ny, own, d_model), BF16),
        pltpu.VMEM((2, nxh, nz, 2, wr, wide), F32),
        pltpu.VMEM((2, nxh, nz, 2, wr, wide), BF16),
        pltpu.VMEM((2, nxh, nz, wr, wide), BF16),
        pltpu.VMEM((2, nxh, nz, wr, wide), BF16),
        pltpu.VMEM((nxx, nz, wr, wide), BF16),
        pltpu.VMEM((nz, wr, wide), BF16),
        pltpu.VMEM((nz, wr, wide), BF16),
        dma((2,)), dma((2, 2)), dma((nyh, 2, 2)), dma((nyh, 2)),
        dma((nz,)), dma((nz,)), dma((nxx,)), dma((nxx,)), dma, dma,
        dma((3,)), dma((2,)), dma((2,)), dma((2,)), dma((2, 2)), dma((2, 2)),
        dma, dma, dma((nxx,)), dma((nxx,)), dma((nz,)), dma((nz,)),
        dma((2 * nyh,)), dma((ny,)),
    ]
    grad_tokens, grad_w = pl.pallas_call(
        functools.partial(kernel, ny, nxh, nz, win, edge),
        out_shape=(
            jax.ShapeDtypeStruct((own, d_model), BF16),
            jax.ShapeDtypeStruct((wr, wide), F32),
        ),
        in_specs=[vmem] * 7 + [pl.BlockSpec(memory_space=pltpu.SMEM), vmem],
        out_specs=(vmem, vmem),
        scratch_shapes=scratch,
        compiler_params=pltpu.CompilerParams(collective_id=0, has_side_effects=True),
    )(
        tokens, cotangent, w_qkv, w_out,
        mod_scale[None, :], mod_shift[None, :], mod_gate[None, :], counts, edge_index,
    )
    grad_qkv = jnp.concatenate([grad_w[:, 2 * HD : 3 * HD], grad_w[:, : 2 * HD]], 1)
    grad_out = grad_w[:, 3 * HD :].T
    return (grad_tokens, grad_qkv, grad_out)


def solution(mesh, nxh=2):
    placed = (
        P(("slab", "enc"), None),
        P(("slab", "enc"), None),
        P("slab", "enc"),
        P("enc", "slab"),
        P(),
        P(),
        P(),
        P("slab"),
        P("slab", None),
    )
    return jax.shard_map(
        functools.partial(on_device, nxh),
        mesh=mesh,
        in_specs=placed,
        out_specs=(P(("slab", "enc"), None), P("slab", "enc"), P("enc", "slab")),
        check_vma=False,
    )
```

time: 281 us -> 91.6 us (0.33)
  waiting for transfers between devices: 116 us -> 0 us
  Pallas kernels: 0 us -> 85.8 us
  blocking collectives: 44.5 us -> 0 us
  matrix products: 40.1 us -> 0 us
  starting transfers between devices: 37.1 us -> 0 us
  other arithmetic: 20.3 us -> 0.69 us
  between operations: 14.4 us -> 0.65 us
    pallas_call x0 -> x1, Pallas kernels: none -> 85.8 us  [on_device(): pl.pallas_call(functools.partial(kernel, ny, nxh, nz, win, edge), out_sha...]
    all_to_all x3 -> x0, waiting for transfers between devices: 62.6 us -> none  [sum_at_owner(): lax.all_to_all(blocks, axis, split_axis=0, concat_axis=0, tiled=True)]
    all_gather x1 -> x0, waiting for transfers between devices: 53.5 us -> none  [in_one_piece(): whole = lax.all_gather(both, axis, axis=dim, tiled=True)]
    all_gather x1 -> x0, blocking collectives: 44.5 us -> none  [turned_gather(): whole = lax.all_gather(both, axis, axis=0, tiled=True)]
    dot_general x10 -> x0, matrix products: 36 us -> none  [the longest x1 8.88 us: attend(): jnp.einsum('wqk,wqd->wkd', grad_score, query_win, preferred_element_type=...]
    all_to_all x3 -> x0, starting transfers between devices: 23.4 us -> none  [sum_at_owner(): lax.all_to_all(blocks, axis, split_axis=0, concat_axis=0, tiled=True)]
    ppermute x3 -> x0, starting transfers between devices: 13.7 us -> none  [shifted(): return lax.ppermute(block, axis, route)]
    reduce_sum x6 -> x0, other arithmetic: 7.23 us -> none  [the longest x1 2.28 us: statistics(): variance = jnp.mean(centred * centred, 1, keepdims=True)]
  transfers between devices with their start and end apart: 7 -> 0, of which waited for: 4 -> 0; matrix products, arithmetic and copies ran while one was open for 9% -> 0% of each run, Pallas kernels for 0% -> 0%
where the time goes in v1:
time: 91.6 us; the launch traced here: 91.4 us
  Pallas kernels  85.8 us (94%)
  local copies, waits for them, and re-layouts  4.27 us (5%)
    pallas_call x1, Pallas kernels, on_device(): pl.pallas_call(functools.partial(kernel, ny, nxh, nz, win, edge), out_sha...  85.8 us
    unnamed x4, local copies, waits for them, and re-layouts  2.05 us

profile of v1, /device:TPU:1, one launch (start us, length us, event | category | flops | bytes accessed | tf_op | source)
XLA Modules:
  0.0 91.4 jit_solution(6242801578410280869)
XLA Ops:
  0.6 1.4 %copy.12.wo = bf16[64,32]{1,0:T(8,128)(2,1)} copy(bf16[64,32]{0,1:T(8,128)(2,1)} %param.12) | data formatting | bytes 8192 | tf_op args[3]
  2.0 85.8 %shard_map.112 = (bf16[64,1024]{1,0:T(8,128)(2,1)}, f32[32,256]{1,0:T(8,128)}) custom-call(bf16[64,1024]{1,0:T(8,128)(2,1)} %tok.1, bf16[64,1024]{1,0:T(8,128)(2,1)} %cot.1, bf16[32,192]{1,0:T(8,128)(2,1)} %wq.1, bf16[64,32]{1,0:T(8,128)(2,1)} %copy.12.wo, f32[1,1024]{1,0:T(1,128)} %bitcast.5, f32[1,1024]{1,0:T(1,128)} %bitcast.6, f32[1,1024]{1,0:T(1,128)} %bitcast.7, ...), custom_call_target="tpu_custom_call" | custom-call | tf_op jit(solution)/shard_map/pallas_call | solution.py:590
  87.8 0.0 copy-start
  87.8 0.8 slice.10
  88.6 1.5 %slice_bitcast_fusion = (f32[64,32]{0,1:T(8,128)}, f32[32,64]{1,0:T(8,128)S(1)}) fusion(f32[32,256]{1,0:T(8,128)} %get-tuple-element.6), kind=kLoop, calls=%fused_computation.1 | loop fusion | bytes 32768 | tf_op jit(solution)/shard_map/transpose | solution.py:605
  90.0 0.7 pad_maximum_fusion
  90.7 0.0 copy-done
  90.7 0.7 copy.14
Async XLA Ops:
  87.8 2.9 %copy-start = (bf16[64,1024]{1,0:T(8,128)(2,1)S(1)}, bf16[64,1024]{1,0:T(8,128)(2,1)}, u32[]{:S(2)}) copy-start(bf16[64,1024]{1,0:T(8,128)(2,1)} %get-tuple-element.12) | copy-start | bytes 393220

commit v2 on v1

--- a/solution.py
+++ b/solution.py
@@ -21,13 +21,14 @@
 
 def kernel(
     ny, nxh, nz, win, edge,
+    tok_in, cot_in, wq_in, wo_in, scale_in, shift_in, gate_in, counts_in, edges_in,
+    out_tok, out_qkv, out_o,
     tok, cot, wq, wo, scale, shift, gate, counts, edges,
-    out_tok, out_w,
     nrm, nx, inv, act, xt, wbuf, meta_nat, meta_own, meta_next,
-    kv, kvt, qa, oh, e_send, e_recv, g_send, g_recv, gkv, gg,
-    pv_send, pv_recv, dwf, dwb, r1, s2, r2, s3, r3,
-    f1s, f1r, f2s, f2r, wzs, wzr, wxs, wxr, wcs, wcr,
-    ms, mr, es, er, gs, gr, dcs, dcr, dxs, dxr, dzs, dzr, ps, pr,
+    kv, kvt, qa, oh, e_send, e_recv, g_send, g_recv, wts, gsc, gkvb, qab,
+    pvf, csd, crv, osd, oself, orv, dwf, dwb, r1, s2, r2, s3, r3,
+    ins, f1s, f1r, f2s, f2r, wzs, wzr, wxs, wxr, wcs, wcr,
+    ms, mr, es, er, gs, gr, dcs, dcr, dxs, dxr, dzs, dzr, ccs, ccr, ows, owr, oss, osr,
 ):
     ns = nxh * nz * 2
     nyh = ny // 2
@@ -36,6 +37,7 @@
     blk = 2 * own
     d_model = tok.shape[1]
     wr = wq.shape[0]
+    halfcol = d_model // 2
 
     enc = lax.axis_index("enc")
     slab = lax.axis_index("slab")
@@ -72,6 +74,30 @@
     at_home = jnp.logical_and(c == xl, half == c)
     away = jnp.logical_not(at_home)
     diag = c == xl
+
+    pending = []
+
+    def launch(make, when=None):
+        if when is None:
+            make().start()
+            pending.append((make, None))
+        else:
+
+            @pl.when(when)
+            def _():
+                make().start()
+
+            pending.append((make, when))
+
+    def drain():
+        for make, when in pending:
+            if when is None:
+                make().wait_send()
+            else:
+
+                @pl.when(when)
+                def _():
+                    make().wait_send()
 
     barrier = pltpu.get_barrier_semaphore()
 
@@ -97,13 +123,38 @@
     def _():
         greet(at(y, xl, xh, z, xl))
 
-    for yy in range(ny):
-
-        @pl.when(jnp.logical_or(away, yy != y))
-        def _():
-            greet(at(yy, c, xh, z, half))
-
-    greeted = 3 + (nz - 1) + (nxx - 1) + 4 + (ny + 1) - 2 * at_home.astype(jnp.int32)
+    above, below = (y + 1) % ny, (y + ny - 1) % ny
+    greet(at(above, c, xh, z, half))
+    greet(at(below, c, xh, z, half))
+
+    @pl.when(away)
+    def _():
+        greet(at(y, c, xh, z, half))
+
+    def count_of(flag):
+        return flag.astype(jnp.int32)
+
+    greeted = (
+        3 + (nz - 1) + (nxx - 1) + 4 + 1
+        - 2 * count_of(at_home)
+        + 2 * count_of(half == c)
+        + 2 * count_of(above // nyh == c)
+        + 2 * count_of(below // nyh == c)
+    )
+
+    arrivals = [
+        pltpu.make_async_copy(src, dst, ins.at[n])
+        for n, (src, dst) in enumerate(
+            (
+                (tok_in, tok), (cot_in, cot), (wq_in, wq), (wo_in, wo), (scale_in, scale),
+                (shift_in, shift), (gate_in, gate), (counts_in, counts), (edges_in, edges),
+            )
+        )
+    ]
+    for arrival in arrivals:
+        arrival.start()
+    for arrival in arrivals:
+        arrival.wait()
 
     widened = tok[...].astype(F32)
     average = jnp.mean(widened, 1, keepdims=True)
@@ -117,13 +168,9 @@
     nrm[0] = (normal * gain + shift[...]).astype(BF16)
     nrm[1] = (cot[...].astype(F32) * gate[...]).astype(BF16)
 
-    hd = wo.shape[0]
-    eye = (
-        lax.broadcasted_iota(jnp.int32, (wr, wr), 0) == lax.broadcasted_iota(jnp.int32, (wr, wr), 1)
-    ).astype(F32).astype(BF16)
-    wo_t = dot(eye, wo[...], ((1,), (1,))).astype(BF16)
+    hd = HD
     wq_here = wq[...]
-    wbuf[xl, xh, z, c] = jnp.concatenate([wq_here[:, hd : 3 * hd], wq_here[:, :hd], wo_t], 1)
+    wbuf[xl, xh, z, c] = jnp.concatenate([wq_here[:, hd : 3 * hd], wq_here[:, :hd], wo[...]], 1)
 
     meta_nat[...] = jnp.zeros(meta_nat.shape, jnp.int32)
     meta_nat[0:2, :] = edges[...]
@@ -154,10 +201,7 @@
         )
 
     for p in range(2):
-
-        @pl.when(away)
-        def _():
-            f1(p).start()
+        launch(functools.partial(f1, p), away)
 
     def wz(j):
         return copy(wbuf.at[xl, xh, z, c], wbuf.at[xl, xh, z, c], wzs.at[j], wzr.at[j], z_peer(j))
@@ -167,17 +211,15 @@
         return copy(block, block, wzs.at[j], wzr.at[j], z_peer(j))
 
     for j in range(1, nz):
-        wz(j).start()
+        launch(functools.partial(wz, j))
 
     def meta_out(n):
         if n == 0:
             return copy(meta_nat, meta_own, ms.at[0], mr.at[0], sibling)
         return copy(meta_nat, meta_next, ms.at[n], mr.at[1], at_slab(before, n - 1))
 
-    @pl.when(diag)
-    def _():
-        for n in range(3):
-            meta_out(n).start()
+    for n in range(3):
+        launch(functools.partial(meta_out, n), diag)
 
     def f1_in(h, p):
         rows = pl.ds(pl.multiple_of((y % nyh) * blk + h * own, own), own)
@@ -190,6 +232,13 @@
         )
 
     here = y % nyh
+    for i in range(nyh):
+        apart = (y + ny - i - nyh * c) % ny
+        back = (ny - apart) % ny
+        pending.append((functools.partial(ring, i, 0, 0), apart < nyh))
+        pending.append((functools.partial(ring, i, 1, 0), apart < nyh - 1))
+        pending.append((functools.partial(ring, i, 1, 1), back < nyh))
+        pending.append((functools.partial(ring, i, 0, 1), back < nyh - 1))
 
     for p in range(2):
         for h in range(2):
@@ -252,12 +301,12 @@
         for j in range(1, nz):
             wz_in(j).wait_recv()
         for j in range(1, nxx):
-            wx(j).start()
+            launch(functools.partial(wx, j))
 
     def weights_core():
         for j in range(1, nxx):
             wx_in(j).wait_recv()
-        wc(c).start()
+        launch(functools.partial(wc, c))
 
     def weights_done():
         wc(1 - c).wait_recv()
@@ -344,7 +393,7 @@
         return copy(e_send.at[k], e_recv.at[k], es.at[k], er.at[k], sibling)
 
     for k in range(2):
-        edge_out(k).start()
+        launch(functools.partial(edge_out, k))
     for k in range(2):
         edge_in(k).wait_recv()
     for h in range(2):
@@ -358,9 +407,7 @@
     count = jnp.where(c == 0, meta_own[2:3, :], meta_own[3:4, :])
     limit = jnp.concatenate([count] * (step // edge), 1)
 
-    def attend(h):
-        gkv[h] = jnp.zeros(gkv.shape[1:], F32)
-
+    def scores_of(h):
         @pl.loop(0, win // step)
         def _(n):
             q_rows = pl.ds(pl.multiple_of(n * step, step), step)
@@ -373,22 +420,12 @@
             scores = jnp.where(key_live, dot(kv[h], query, ((1,), (1,))), NEG)
             exponent = jnp.exp(scores - jnp.max(scores, 0, keepdims=True))
             probs = exponent * (1.0 / jnp.sum(exponent, 0, keepdims=True))
-            weights = probs.astype(BF16)
+            wts[h, :, q_rows] = probs.astype(BF16)
             g_prob = dot(kv[h], g_att, ((1,), (1,)))
             centre = jnp.sum(g_prob * probs, 0, keepdims=True)
-            g_score = (probs * (g_prob - centre)).astype(BF16)
-            lane = lax.broadcasted_iota(jnp.int32, (HD, step), 1) + n * step
-            attended = jnp.where(lane < limit, dot(kvt[h, HD:, :], weights), 0.0)
-            g_query = dot(kvt[h, :HD, :], g_score) * (HD**-0.5)
-            pair = jnp.concatenate([g_query, attended], 0).T
-            side = lax.broadcasted_iota(jnp.int32, (step, 2 * HD), 1)
-            gg[h, q_rows, 2 * HD :] = jnp.where(side < HD, pair, 0.0).astype(BF16)
-            low = pl.ds(pl.multiple_of(win + n * step, step), step)
-            gg[h, low, 2 * HD :] = jnp.where(side >= HD, pair, 0.0).astype(BF16)
-            gg[h, low, : 2 * HD] = jnp.zeros((step, 2 * HD), BF16)
-            gkv[h] += dot(g_score, query) + dot(weights, g_att)
-
-        g_send[h] = gkv[h, win:, :].astype(BF16)
+            gsc[h, :, q_rows] = (probs * (g_prob - centre)).astype(BF16)
+
+        g_send[h] = (dot(gsc[h, win:, :], qa[h, 0]) + dot(wts[h, win:, :], qa[h, 1])).astype(BF16)
 
     def grad_out(h, k):
         return copy(g_send.at[h], g_recv.at[h, c], gs.at[h, k], gr.at[h, c], at_slab(before, k))
@@ -397,52 +434,110 @@
         return copy(g_send.at[h], g_recv.at[h, k], gs.at[h, k], gr.at[h, k], sibling)
 
     for h in range(2):
-        attend(h)
+        scores_of(h)
         for k in range(2):
-            grad_out(h, k).start()
-    for h in range(2):
+            launch(functools.partial(grad_out, h, k))
+
+    row_limit = jnp.concatenate([count] * (win // edge), 1)
+    lane = lax.broadcasted_iota(jnp.int32, (HD, win), 1)
+    side = lax.broadcasted_iota(jnp.int32, (win, 2 * HD), 1)
+    for h in range(2):
+        cols = pl.ds(h * 2 * HD, 2 * HD)
+        attended = jnp.where(lane < row_limit, dot(kvt[h, HD:, :], wts[h]), 0.0)
+        g_query = dot(kvt[h, :HD, :], gsc[h]) * (HD**-0.5)
+        pair = jnp.concatenate([g_query, attended], 0).T
+        qab[:win, cols] = jnp.where(side < HD, pair, 0.0).astype(BF16)
+        qab[win:, cols] = jnp.where(side >= HD, pair, 0.0).astype(BF16)
+    grad_w = dot(xt[...], qab[...]).reshape(nxh, nz, 2, wr, 4 * HD)
+    for h in range(2):
+        dwf[h, :, :, :, :, 2 * HD :] = grad_w[:, :, :, :, h * 2 * HD : (h + 1) * 2 * HD]
+
+    for h in range(2):
+        cols = pl.ds(h * 2 * HD, 2 * HD)
+        own_pair = dot(gsc[h, :win, :], qa[h, 0]) + dot(wts[h, :win, :], qa[h, 1])
         for k in range(2):
             grad_in(h, k).wait_recv()
         returned = dot(oh[...], g_recv[h].reshape(2 * edge, 2 * HD))
-        gg[h, :win, : 2 * HD] = (gkv[h, :win, :] + returned).astype(BF16)
-
-    def part_out(j):
-        yy = nyh * c + j // 2
-        return copy(pv_send.at[j], pv_recv.at[y], ps.at[j], pr.at[y], at(yy, j % 2, xh, z, xl))
-
-    def part_in(yy):
-        return copy(pv_send.at[0], pv_recv.at[yy], ps.at[0], pr.at[yy], sibling)
-
-    def is_mine(j):
-        return jnp.logical_and(at_home, enc == 2 * nyh * c + j)
+        gkvb[:, cols] = (own_pair + returned).astype(BF16)
+
+    def hops(way, part):
+        return nyh if way == part else nyh - 1
+
+    def chain_link(way, part, i):
+        return copy(
+            csd.at[way, part, i], crv.at[way, part, i], ccs.at[way, part, i], ccr.at[way, part, i],
+            up if way == 0 else down,
+        )
+
+    def chain_end(way, part, i, h, yy):
+        return copy(
+            csd.at[way, part, i, pl.ds(h * own, own)], orv.at[way, part],
+            ows.at[way, part, h], owr.at[way, part], at(yy, h, xh, z, xl),
+        )
+
+    def own_out(h):
+        return copy(osd.at[h], oself, oss.at[h], osr, at(y, h, xh, z, xl))
+
+    def chain(r):
+        for way in range(2):
+            yy = (y + (r if way == 0 else ny - r)) % ny
+            i = (yy + ny - nyh * c) % ny
+            held = i < nyh
+            for part in (way, 1 - way):
+                if r > hops(way, part):
+                    continue
+
+                @pl.when(held)
+                def _():
+                    total = pvf[i, :, part * halfcol : (part + 1) * halfcol]
+                    if r < hops(way, part):
+                        chain_link(way, part, i).wait_recv()
+                        total += crv[way, part, i].astype(F32)
+                    csd[way, part, i] = total.astype(BF16)
+
+                if r > 1:
+                    launch(functools.partial(chain_link, way, part, i), held)
+                else:
+                    for h in range(2):
+                        launch(functools.partial(chain_end, way, part, i, h, yy), held)
 
     for b in range(nyh):
         rows = pl.ds(b * blk, blk)
         total = jnp.zeros((blk, d_model), F32)
         for h in range(2):
-            total += dot(gg[h, rows, :], wbuf[h].reshape(d_model, 4 * HD), ((1,), (1,)))
-        value = total.astype(BF16)
-        for k in range(2):
-            j = 2 * b + k
-            pv_send[j] = value[k * own : (k + 1) * own, :]
-
-            @pl.when(jnp.logical_not(is_mine(j)))
-            def _():
-                part_out(j).start()
-
-            @pl.when(is_mine(j))
-            def _():
-                pv_recv[y] = pv_send[j]
-
-    for h in range(2):
-        grad_w = dot(xt[...], gg[h]).reshape(nxh, nz, 2, wr, 4 * HD)
-        dwf[h] = grad_w
-        dwb[h] = grad_w.astype(BF16)
+            cols = pl.ds(h * 2 * HD, 2 * HD)
+            both = jnp.concatenate([gkvb[rows, cols], qab[rows, cols]], 1)
+            total += dot(both, wbuf[h].reshape(d_model, 4 * HD), ((1,), (1,)))
+        pvf[b] = total
+
+    chain(nyh)
+
+    @pl.when(half == c)
+    def _():
+        for h in range(2):
+            osd[h] = pvf[here, h * own : (h + 1) * own, :].astype(BF16)
+
+    for h in range(2):
+        launch(
+            functools.partial(own_out, h),
+            jnp.logical_and(half == c, jnp.logical_or(xl != c, h != xl)),
+        )
+
+    @pl.when(at_home)
+    def _():
+        oself[...] = osd[xl]
+
+    grad_w = dot(xt[:, :win], gkvb[...]).reshape(nxh, nz, 2, wr, 4 * HD)
+    for h in range(2):
+        dwf[h, :, :, :, :, : 2 * HD] = grad_w[:, :, :, :, h * 2 * HD : (h + 1) * 2 * HD]
+        dwb[h] = dwf[h].astype(BF16)
 
     def dc(k):
         return copy(dwb.at[:, :, :, k], r1, dcs, dcr, sibling)
 
-    dc(1 - c).start()
+    launch(functools.partial(dc, 1 - c))
+    if nyh > 1:
+        chain(nyh - 1)
     dc(1 - c).wait_recv()
     for h in range(2):
         s2[h] = (dwf[h, :, :, c] + r1[h].astype(F32)).astype(BF16)
@@ -452,7 +547,9 @@
         return copy(s2.at[xx % 2, xx // 2], r2.at[j], dxs.at[j], dxr.at[j], x_peer(j))
 
     for j in range(1, nxx):
-        dx(j).start()
+        launch(functools.partial(dx, j))
+    for r in range(nyh - 2, 0, -1):
+        chain(r)
     total = dwf[xl, xh, :, c] + r1[xl, xh].astype(F32)
     for j in range(1, nxx):
         dx(j).wait_recv()
@@ -464,22 +561,26 @@
         return copy(s3.at[(z + j) % nz], r3.at[j], dzs.at[j], dzr.at[j], z_peer(j))
 
     for j in range(1, nz):
-        dz(j).start()
-    final = dwf[0, 0, z, 0]
-    for j in range(1, nz):
-        dz(j).wait_recv()
-        final += r3[j].astype(F32)
-    out_w[...] = final
-
-    mine_sum = jnp.zeros((own, d_model), F32)
-    for yy in range(ny):
-
-        @pl.when(jnp.logical_or(away, yy != y))
-        def _():
-            part_in(yy).wait_recv()
-
-    for yy in range(ny):
-        mine_sum += pv_recv[yy].astype(F32)
+        launch(functools.partial(dz, j))
+
+    def owner_in(way, part):
+        return copy(
+            csd.at[way, part, 0, pl.ds(0, own)], orv.at[way, part],
+            ows.at[way, part, 0], owr.at[way, part], sibling,
+        )
+
+    for way in range(2):
+        for part in range(2):
+            owner_in(way, part).wait_recv()
+
+    @pl.when(away)
+    def _():
+        own_out_arrived = copy(osd.at[0], oself, oss.at[0], osr, sibling)
+        own_out_arrived.wait_recv()
+
+    mine_sum = oself[...].astype(F32) + jnp.concatenate(
+        [orv[0, part].astype(F32) + orv[1, part].astype(F32) for part in range(2)], 1
+    )
     g_hat = mine_sum * gain
     normal_own = nx[...]
     g_tok = cot[...].astype(F32) + inv[:, 0:1] * (
@@ -489,56 +590,14 @@
     )
     out_tok[...] = g_tok.astype(BF16)
 
-    for p in range(2):
-
-        @pl.when(away)
-        def _():
-            f1(p).wait_send()
-
+    final = dwf[0, 0, z, 0]
     for j in range(1, nz):
-        wz(j).wait_send()
-        dz(j).wait_send()
-    for j in range(1, nxx):
-        wx(j).wait_send()
-        dx(j).wait_send()
-    wc(c).wait_send()
-    dc(1 - c).wait_send()
-
-    @pl.when(diag)
-    def _():
-        for n in range(3):
-            meta_out(n).wait_send()
-
-    for i in range(nyh):
-        apart = (y + ny - i - nyh * c) % ny
-
-        @pl.when(apart < nyh)
-        def _():
-            ring(i, 0, 0).wait_send()
-
-        @pl.when(apart < nyh - 1)
-        def _():
-            ring(i, 1, 0).wait_send()
-
-        back = (ny - apart) % ny
-
-        @pl.when(back < nyh)
-        def _():
-            ring(i, 1, 1).wait_send()
-
-        @pl.when(back < nyh - 1)
-        def _():
-            ring(i, 0, 1).wait_send()
-
-    for k in range(2):
-        edge_out(k).wait_send()
-        for h in range(2):
-            grad_out(h, k).wait_send()
-    for j in range(2 * nyh):
-
-        @pl.when(jnp.logical_not(is_mine(j)))
-        def _():
-            part_out(j).wait_send()
+        dz(j).wait_recv()
+        final += r3[j].astype(F32)
+    out_qkv[...] = jnp.concatenate([final[:, 2 * HD : 3 * HD], final[:, : 2 * HD]], 1)
+    out_o[...] = final[:, 3 * HD :]
+
+    drain()
 
 
 def on_device(nxh, tokens, cotangent, w_qkv, w_out, mod_scale, mod_shift, mod_gate, counts, edge_index):
@@ -552,7 +611,19 @@
     wide = 4 * HD
     dma = pltpu.SemaphoreType.DMA
     vmem = pl.BlockSpec(memory_space=pltpu.VMEM)
+    anywhere = pl.BlockSpec(memory_space=pl.ANY)
+    keys = win + edge
+    blk = 2 * own
     scratch = [
+        pltpu.VMEM((own, d_model), BF16),
+        pltpu.VMEM((own, d_model), BF16),
+        pltpu.VMEM((wr, 3 * HD), BF16),
+        pltpu.VMEM((wr, HD), BF16),
+        pltpu.VMEM((1, d_model), F32),
+        pltpu.VMEM((1, d_model), F32),
+        pltpu.VMEM((1, d_model), F32),
+        pltpu.SMEM((2,), jnp.int32),
+        pltpu.VMEM((2, edge), jnp.int32),
         pltpu.VMEM((2, own, d_model), BF16),
         pltpu.VMEM((own, d_model), F32),
         pltpu.VMEM((own, 128), F32),
@@ -562,18 +633,24 @@
         pltpu.VMEM((8, edge), jnp.int32),
         pltpu.VMEM((8, edge), jnp.int32),
         pltpu.VMEM((8, edge), jnp.int32),
-        pltpu.VMEM((2, win + edge, 2 * HD), BF16),
-        pltpu.VMEM((2, 2 * HD, win + edge), BF16),
+        pltpu.VMEM((2, keys, 2 * HD), BF16),
+        pltpu.VMEM((2, 2 * HD, keys), BF16),
         pltpu.VMEM((2, 2, win, 2 * HD), BF16),
         pltpu.VMEM((win, 2 * edge), BF16),
         pltpu.VMEM((2, 2, 2 * HD, edge), BF16),
         pltpu.VMEM((2, 2, 2 * HD, edge), BF16),
         pltpu.VMEM((2, edge, 2 * HD), BF16),
         pltpu.VMEM((2, 2, edge, 2 * HD), BF16),
-        pltpu.VMEM((2, win + edge, 2 * HD), F32),
-        pltpu.VMEM((2, 2 * win, wide), BF16),
-        pltpu.VMEM((2 * nyh, own, d_model), BF16),
-        pltpu.VMEM((ny, own, d_model), BF16),
+        pltpu.VMEM((2, keys, win), BF16),
+        pltpu.VMEM((2, keys, win), BF16),
+        pltpu.VMEM((win, wide), BF16),
+        pltpu.VMEM((2 * win, wide), BF16),
+        pltpu.VMEM((nyh, blk, d_model), F32),
+        pltpu.VMEM((2, 2, nyh, blk, d_model // 2), BF16),
+        pltpu.VMEM((2, 2, nyh, blk, d_model // 2), BF16),
+        pltpu.VMEM((2, own, d_model), BF16),
+        pltpu.VMEM((own, d_model), BF16),
+        pltpu.VMEM((2, 2, own, d_model // 2), BF16),
         pltpu.VMEM((2, nxh, nz, 2, wr, wide), F32),
         pltpu.VMEM((2, nxh, nz, 2, wr, wide), BF16),
         pltpu.VMEM((2, nxh, nz, wr, wide), BF16),
@@ -581,29 +658,29 @@
         pltpu.VMEM((nxx, nz, wr, wide), BF16),
         pltpu.VMEM((nz, wr, wide), BF16),
         pltpu.VMEM((nz, wr, wide), BF16),
+        dma((9,)),
         dma((2,)), dma((2, 2)), dma((nyh, 2, 2)), dma((nyh, 2)),
         dma((nz,)), dma((nz,)), dma((nxx,)), dma((nxx,)), dma, dma,
         dma((3,)), dma((2,)), dma((2,)), dma((2,)), dma((2, 2)), dma((2, 2)),
         dma, dma, dma((nxx,)), dma((nxx,)), dma((nz,)), dma((nz,)),
-        dma((2 * nyh,)), dma((ny,)),
+        dma((2, 2, nyh)), dma((2, 2, nyh)), dma((2, 2, 2)), dma((2, 2)), dma((2,)), dma,
     ]
-    grad_tokens, grad_w = pl.pallas_call(
+    grad_tokens, grad_qkv, grad_out = pl.pallas_call(
         functools.partial(kernel, ny, nxh, nz, win, edge),
         out_shape=(
             jax.ShapeDtypeStruct((own, d_model), BF16),
-            jax.ShapeDtypeStruct((wr, wide), F32),
+            jax.ShapeDtypeStruct((wr, 3 * HD), F32),
+            jax.ShapeDtypeStruct((wr, HD), F32),
         ),
-        in_specs=[vmem] * 7 + [pl.BlockSpec(memory_space=pltpu.SMEM), vmem],
-        out_specs=(vmem, vmem),
+        in_specs=[anywhere] * 9,
+        out_specs=(vmem, vmem, vmem),
         scratch_shapes=scratch,
         compiler_params=pltpu.CompilerParams(collective_id=0, has_side_effects=True),
     )(
-        tokens, cotangent, w_qkv, w_out,
+        tokens, cotangent, w_qkv, w_out.T,
         mod_scale[None, :], mod_shift[None, :], mod_gate[None, :], counts, edge_index,
     )
-    grad_qkv = jnp.concatenate([grad_w[:, 2 * HD : 3 * HD], grad_w[:, : 2 * HD]], 1)
-    grad_out = grad_w[:, 3 * HD :].T
-    return (grad_tokens, grad_qkv, grad_out)
+    return (grad_tokens, grad_qkv, grad_out.T)
 
 
 def solution(mesh, nxh=2):

time: 91.6 us -> 82 us (0.90)
  Pallas kernels: 85.8 us -> 77.4 us
  local copies, waits for them, and re-layouts: 4.27 us -> 2.91 us
    pallas_call x1, Pallas kernels: 85.8 us -> 77.4 us  [on_device(): pl.pallas_call(functools.partial(kernel, ny, nxh, nz, win, edge), out_sha...]
    transpose x1 -> x0, local copies, waits for them, and re-layouts: 1.47 us -> none  [on_device(): grad_out = grad_w[:, 3 * HD:].T]
    unnamed x4 -> x7, local copies, waits for them, and re-layouts: 2.05 us -> 2.91 us
where the time goes in v2:
time: 82 us; the launch traced here: 81 us
  Pallas kernels  77.4 us (94%)
  local copies, waits for them, and re-layouts  2.91 us (4%)
    pallas_call x1, Pallas kernels, on_device(): pl.pallas_call(functools.partial(kernel, ny, nxh, nz, win, edge), out_sha...  77.4 us
    unnamed x7, local copies, waits for them, and re-layouts  2.91 us

profile of v2, /device:TPU:1, one launch (start us, length us, event | category | flops | bytes accessed | tf_op | source)
XLA Modules:
  0.0 81.0 jit_solution(2802321335013053867)
XLA Ops:
  0.6 77.4 %shard_map.112 = (bf16[64,1024]{1,0:T(8,128)(2,1)}, f32[32,192]{1,0:T(8,128)}, f32[32,64]{1,0:T(8,128)}) custom-call(bf16[64,1024]{1,0:T(8,128)(2,1)} %tok_in.1, bf16[64,1024]{1,0:T(8,128)(2,1)} %cot_in.1, bf16[32,192]{1,0:T(8,128)(2,1)} %wq_in.1, bf16[32,64]{1,0:T(8,128)(2,1)} %bitcast.6, f32[1,1024]{1,0:T(1,128)} %bitcast.7, f32[1,1024]{1,0:T(1,128)} %bitcast.8, ...), custom_call_target="tpu_custom_call" | custom-call | tf_op jit(solution)/shard_map/pallas_call | solution.py:668
  78.0 0.0 copy-start
  78.0 1.6 %copy.15 = bf16[64,1024]{1,0:T(8,128)(2,1)} copy(bf16[64,1024]{1,0:T(8,128)(2,1)} %get-tuple-element.12) | data formatting | bytes 262144
  79.6 0.0 copy-done
  79.6 0.0 copy-start.1
  79.6 0.6 copy.16
  80.2 0.1 copy-done.1
  80.4 0.6 copy.17
Async XLA Ops:
  78.0 1.6 %copy-start = (f32[32,192]{1,0:T(8,128)S(1)}, f32[32,192]{1,0:T(8,128)}, u32[]{:S(2)}) copy-start(f32[32,192]{1,0:T(8,128)} %get-tuple-element.13) | copy-start | bytes 73732
  79.6 0.7 copy-start.1

commit v3 on v2

--- a/solution.py
+++ b/solution.py
@@ -25,8 +25,8 @@
     out_tok, out_qkv, out_o,
     tok, cot, wq, wo, scale, shift, gate, counts, edges,
     nrm, nx, inv, act, xt, wbuf, meta_nat, meta_own, meta_next,
-    kv, kvt, qa, oh, e_send, e_recv, g_send, g_recv, wts, gsc, gkvb, qab,
-    pvf, csd, crv, osd, oself, orv, dwf, dwb, r1, s2, r2, s3, r3,
+    kv, kvt, qa, oh, e_send, e_recv, g_send, g_recv, wts, gsc, part_e, part_g, stat, gkvb, qab,
+    pvf, csd, crv, osd, oself, orv, dwf, dwb, r1, s2, r2, tot, s3, r3,
     ins, f1s, f1r, f2s, f2r, wzs, wzr, wxs, wxr, wcs, wcr,
     ms, mr, es, er, gs, gr, dcs, dcr, dxs, dxr, dzs, dzr, ccs, ccr, ows, owr, oss, osr,
 ):
@@ -394,6 +394,29 @@
 
     for k in range(2):
         launch(functools.partial(edge_out, k))
+    keys = win + edge
+    step = 256 if win % 256 == 0 else win
+    has_edge = mine > 0
+    count = jnp.where(c == 0, meta_own[2:3, :], meta_own[3:4, :])
+    limit = jnp.concatenate([count] * (step // edge), 1)
+
+    for h in range(2):
+
+        @pl.loop(0, win // step)
+        def _(n):
+            q_rows = pl.ds(pl.multiple_of(n * step, step), step)
+            key_live = lax.broadcasted_iota(jnp.int32, (win, step), 0) < limit
+            scores = dot(kv[h, :win, :], qa[h, 0, q_rows, :], ((1,), (1,)))
+            scores = jnp.where(key_live, scores, NEG)
+            largest = jnp.max(scores, 0, keepdims=True)
+            exponent = jnp.exp(scores - largest)
+            g_prob = dot(kv[h, :win, :], qa[h, 1, q_rows, :], ((1,), (1,)))
+            part_e[h, :, q_rows] = exponent
+            part_g[h, :, q_rows] = g_prob
+            stat[h, 0:1, q_rows] = largest
+            stat[h, 1:2, q_rows] = jnp.sum(exponent, 0, keepdims=True)
+            stat[h, 2:3, q_rows] = jnp.sum(exponent * g_prob, 0, keepdims=True)
+
     for k in range(2):
         edge_in(k).wait_recv()
     for h in range(2):
@@ -401,29 +424,27 @@
         kvt[h, :, win:] = arrived.astype(BF16)
         kv[h, win:, :] = arrived.T.astype(BF16)
 
-    keys = win + edge
-    step = 256 if win % 256 == 0 else win
-    has_edge = mine > 0
-    count = jnp.where(c == 0, meta_own[2:3, :], meta_own[3:4, :])
-    limit = jnp.concatenate([count] * (step // edge), 1)
-
     def scores_of(h):
         @pl.loop(0, win // step)
         def _(n):
             q_rows = pl.ds(pl.multiple_of(n * step, step), step)
-            query = qa[h, 0, q_rows, :]
-            g_att = qa[h, 1, q_rows, :]
-            key_id = lax.broadcasted_iota(jnp.int32, (keys, step), 0)
-            key_live = jnp.logical_or(
-                key_id < limit, jnp.logical_and(key_id >= win, has_edge)
+            scores = dot(kv[h, win:, :], qa[h, 0, q_rows, :], ((1,), (1,)))
+            scores = jnp.where(has_edge, scores, NEG)
+            own_largest = stat[h, 0:1, q_rows]
+            largest = jnp.maximum(own_largest, jnp.max(scores, 0, keepdims=True))
+            exponent = jnp.exp(scores - largest)
+            g_prob = dot(kv[h, win:, :], qa[h, 1, q_rows, :], ((1,), (1,)))
+            shrink = jnp.exp(own_largest - largest)
+            norm = 1.0 / (shrink * stat[h, 1:2, q_rows] + jnp.sum(exponent, 0, keepdims=True))
+            centre = norm * (
+                shrink * stat[h, 2:3, q_rows] + jnp.sum(exponent * g_prob, 0, keepdims=True)
             )
-            scores = jnp.where(key_live, dot(kv[h], query, ((1,), (1,))), NEG)
-            exponent = jnp.exp(scores - jnp.max(scores, 0, keepdims=True))
-            probs = exponent * (1.0 / jnp.sum(exponent, 0, keepdims=True))
-            wts[h, :, q_rows] = probs.astype(BF16)
-            g_prob = dot(kv[h], g_att, ((1,), (1,)))
-            centre = jnp.sum(g_prob * probs, 0, keepdims=True)
-            gsc[h, :, q_rows] = (probs * (g_prob - centre)).astype(BF16)
+            probs = exponent * norm
+            wts[h, win:, q_rows] = probs.astype(BF16)
+            gsc[h, win:, q_rows] = (probs * (g_prob - centre)).astype(BF16)
+            own_probs = part_e[h, :, q_rows] * (shrink * norm)
+            wts[h, :win, q_rows] = own_probs.astype(BF16)
+            gsc[h, :win, q_rows] = (own_probs * (part_g[h, :, q_rows] - centre)).astype(BF16)
 
         g_send[h] = (dot(gsc[h, win:, :], qa[h, 0]) + dot(wts[h, win:, :], qa[h, 1])).astype(BF16)
 
@@ -448,9 +469,46 @@
         pair = jnp.concatenate([g_query, attended], 0).T
         qab[:win, cols] = jnp.where(side < HD, pair, 0.0).astype(BF16)
         qab[win:, cols] = jnp.where(side >= HD, pair, 0.0).astype(BF16)
-    grad_w = dot(xt[...], qab[...]).reshape(nxh, nz, 2, wr, 4 * HD)
-    for h in range(2):
-        dwf[h, :, :, :, :, 2 * HD :] = grad_w[:, :, :, :, h * 2 * HD : (h + 1) * 2 * HD]
+
+    def dc(q, k):
+        return copy(dwb.at[q, :, :, :, k], r1.at[q], dcs.at[q], dcr.at[q], sibling)
+
+    def dx(q, j):
+        xx = (x + j) % nxx
+        return copy(
+            s2.at[q, xx % 2, xx // 2], r2.at[q, j], dxs.at[q, j], dxr.at[q, j], x_peer(j)
+        )
+
+    def dz(j):
+        return copy(s3.at[(z + j) % nz], r3.at[j], dzs.at[j], dzr.at[j], z_peer(j))
+
+    def weights_start(q, grad_w):
+        blocks = grad_w.reshape(nxh, nz, 2, wr, 4 * HD)
+        for h in range(2):
+            block = blocks[:, :, :, :, h * 2 * HD : (h + 1) * 2 * HD]
+            dwf[q, h] = block
+            dwb[q, h] = block.astype(BF16)
+        launch(functools.partial(dc, q, 1 - c))
+
+    def weights_cross(q):
+        dc(q, 1 - c).wait_recv()
+        for h in range(2):
+            s2[q, h] = (dwf[q, h, :, :, c] + r1[q, h].astype(F32)).astype(BF16)
+        for j in range(1, nxx):
+            launch(functools.partial(dx, q, j))
+
+    def weights_spread():
+        for q in (1, 0):
+            total = dwf[q, xl, xh, :, c] + r1[q, xl, xh].astype(F32)
+            for j in range(1, nxx):
+                dx(q, j).wait_recv()
+                total += r2[q, j].astype(F32)
+            tot[:, q] = total
+            s3[:, q] = total.astype(BF16)
+        for j in range(1, nz):
+            launch(functools.partial(dz, j))
+
+    weights_start(1, dot(xt[...], qab[...]))
 
     for h in range(2):
         cols = pl.ds(h * 2 * HD, 2 * HD)
@@ -460,46 +518,51 @@
         returned = dot(oh[...], g_recv[h].reshape(2 * edge, 2 * HD))
         gkvb[:, cols] = (own_pair + returned).astype(BF16)
 
+    weights_cross(1)
+
     def hops(way, part):
         return nyh if way == part else nyh - 1
 
-    def chain_link(way, part, i):
+    def chain_link(way, part, i, h):
         return copy(
-            csd.at[way, part, i], crv.at[way, part, i], ccs.at[way, part, i], ccr.at[way, part, i],
-            up if way == 0 else down,
+            csd.at[way, part, i, h], crv.at[way, part, i, h],
+            ccs.at[way, part, i, h], ccr.at[way, part, i, h], up if way == 0 else down,
         )
 
     def chain_end(way, part, i, h, yy):
         return copy(
-            csd.at[way, part, i, pl.ds(h * own, own)], orv.at[way, part],
+            csd.at[way, part, i, h], orv.at[way, part],
             ows.at[way, part, h], owr.at[way, part], at(yy, h, xh, z, xl),
         )
 
     def own_out(h):
         return copy(osd.at[h], oself, oss.at[h], osr, at(y, h, xh, z, xl))
 
+    def chain_part(way, part, r):
+        yy = (y + (r if way == 0 else ny - r)) % ny
+        i = (yy + ny - nyh * c) % ny
+        held = i < nyh
+        for h in range(2):
+
+            @pl.when(held)
+            def _():
+                total = pvf[i, h * own : (h + 1) * own, part * halfcol : (part + 1) * halfcol]
+                if r < hops(way, part):
+                    chain_link(way, part, i, h).wait_recv()
+                    total += crv[way, part, i, h].astype(F32)
+                csd[way, part, i, h] = total.astype(BF16)
+
+            if r > 1:
+                launch(functools.partial(chain_link, way, part, i, h), held)
+            else:
+                launch(functools.partial(chain_end, way, part, i, h, yy), held)
+
     def chain(r):
         for way in range(2):
-            yy = (y + (r if way == 0 else ny - r)) % ny
-            i = (yy + ny - nyh * c) % ny
-            held = i < nyh
-            for part in (way, 1 - way):
-                if r > hops(way, part):
-                    continue
-
-                @pl.when(held)
-                def _():
-                    total = pvf[i, :, part * halfcol : (part + 1) * halfcol]
-                    if r < hops(way, part):
-                        chain_link(way, part, i).wait_recv()
-                        total += crv[way, part, i].astype(F32)
-                    csd[way, part, i] = total.astype(BF16)
-
-                if r > 1:
-                    launch(functools.partial(chain_link, way, part, i), held)
-                else:
-                    for h in range(2):
-                        launch(functools.partial(chain_end, way, part, i, h, yy), held)
+            chain_part(way, way, r)
+        if r > 1:
+            for way in range(2):
+                chain_part(way, 1 - way, r - 1)
 
     for b in range(nyh):
         rows = pl.ds(b * blk, blk)
@@ -527,45 +590,17 @@
     def _():
         oself[...] = osd[xl]
 
-    grad_w = dot(xt[:, :win], gkvb[...]).reshape(nxh, nz, 2, wr, 4 * HD)
-    for h in range(2):
-        dwf[h, :, :, :, :, : 2 * HD] = grad_w[:, :, :, :, h * 2 * HD : (h + 1) * 2 * HD]
-        dwb[h] = dwf[h].astype(BF16)
-
-    def dc(k):
-        return copy(dwb.at[:, :, :, k], r1, dcs, dcr, sibling)
-
-    launch(functools.partial(dc, 1 - c))
-    if nyh > 1:
-        chain(nyh - 1)
-    dc(1 - c).wait_recv()
-    for h in range(2):
-        s2[h] = (dwf[h, :, :, c] + r1[h].astype(F32)).astype(BF16)
-
-    def dx(j):
-        xx = (x + j) % nxx
-        return copy(s2.at[xx % 2, xx // 2], r2.at[j], dxs.at[j], dxr.at[j], x_peer(j))
-
-    for j in range(1, nxx):
-        launch(functools.partial(dx, j))
-    for r in range(nyh - 2, 0, -1):
+    weights_start(0, dot(xt[:, :win], gkvb[...]))
+    for r in range(nyh - 1, 0, -1):
+        if r == 1:
+            weights_spread()
         chain(r)
-    total = dwf[xl, xh, :, c] + r1[xl, xh].astype(F32)
-    for j in range(1, nxx):
-        dx(j).wait_recv()
-        total += r2[j].astype(F32)
-    dwf[0, 0, :, 0] = total
-    s3[...] = total.astype(BF16)
-
-    def dz(j):
-        return copy(s3.at[(z + j) % nz], r3.at[j], dzs.at[j], dzr.at[j], z_peer(j))
-
-    for j in range(1, nz):
-        launch(functools.partial(dz, j))
+        if r == nyh - 1:
+            weights_cross(0)
 
     def owner_in(way, part):
         return copy(
-            csd.at[way, part, 0, pl.ds(0, own)], orv.at[way, part],
+            csd.at[way, part, 0, 0], orv.at[way, part],
             ows.at[way, part, 0], owr.at[way, part], sibling,
         )
 
@@ -590,12 +625,12 @@
     )
     out_tok[...] = g_tok.astype(BF16)
 
-    final = dwf[0, 0, z, 0]
+    final = tot[z]
     for j in range(1, nz):
         dz(j).wait_recv()
         final += r3[j].astype(F32)
-    out_qkv[...] = jnp.concatenate([final[:, 2 * HD : 3 * HD], final[:, : 2 * HD]], 1)
-    out_o[...] = final[:, 3 * HD :]
+    out_qkv[...] = jnp.concatenate([final[1, :, :HD], final[0]], 1)
+    out_o[...] = final[1, :, HD:]
 
     drain()
 
@@ -643,27 +678,31 @@
         pltpu.VMEM((2, 2, edge, 2 * HD), BF16),
         pltpu.VMEM((2, keys, win), BF16),
         pltpu.VMEM((2, keys, win), BF16),
+        pltpu.VMEM((2, win, win), F32),
+        pltpu.VMEM((2, win, win), F32),
+        pltpu.VMEM((2, 8, win), F32),
         pltpu.VMEM((win, wide), BF16),
         pltpu.VMEM((2 * win, wide), BF16),
         pltpu.VMEM((nyh, blk, d_model), F32),
-        pltpu.VMEM((2, 2, nyh, blk, d_model // 2), BF16),
-        pltpu.VMEM((2, 2, nyh, blk, d_model // 2), BF16),
+        pltpu.VMEM((2, 2, nyh, 2, own, d_model // 2), BF16),
+        pltpu.VMEM((2, 2, nyh, 2, own, d_model // 2), BF16),
         pltpu.VMEM((2, own, d_model), BF16),
         pltpu.VMEM((own, d_model), BF16),
         pltpu.VMEM((2, 2, own, d_model // 2), BF16),
-        pltpu.VMEM((2, nxh, nz, 2, wr, wide), F32),
-        pltpu.VMEM((2, nxh, nz, 2, wr, wide), BF16),
-        pltpu.VMEM((2, nxh, nz, wr, wide), BF16),
-        pltpu.VMEM((2, nxh, nz, wr, wide), BF16),
-        pltpu.VMEM((nxx, nz, wr, wide), BF16),
-        pltpu.VMEM((nz, wr, wide), BF16),
-        pltpu.VMEM((nz, wr, wide), BF16),
+        pltpu.VMEM((2, 2, nxh, nz, 2, wr, 2 * HD), F32),
+        pltpu.VMEM((2, 2, nxh, nz, 2, wr, 2 * HD), BF16),
+        pltpu.VMEM((2, 2, nxh, nz, wr, 2 * HD), BF16),
+        pltpu.VMEM((2, 2, nxh, nz, wr, 2 * HD), BF16),
+        pltpu.VMEM((2, nxx, nz, wr, 2 * HD), BF16),
+        pltpu.VMEM((nz, 2, wr, 2 * HD), F32),
+        pltpu.VMEM((nz, 2, wr, 2 * HD), BF16),
+        pltpu.VMEM((nz, 2, wr, 2 * HD), BF16),
         dma((9,)),
         dma((2,)), dma((2, 2)), dma((nyh, 2, 2)), dma((nyh, 2)),
         dma((nz,)), dma((nz,)), dma((nxx,)), dma((nxx,)), dma, dma,
         dma((3,)), dma((2,)), dma((2,)), dma((2,)), dma((2, 2)), dma((2, 2)),
-        dma, dma, dma((nxx,)), dma((nxx,)), dma((nz,)), dma((nz,)),
-        dma((2, 2, nyh)), dma((2, 2, nyh)), dma((2, 2, 2)), dma((2, 2)), dma((2,)), dma,
+        dma((2,)), dma((2,)), dma((2, nxx)), dma((2, nxx)), dma((nz,)), dma((nz,)),
+        dma((2, 2, nyh, 2)), dma((2, 2, nyh, 2)), dma((2, 2, 2)), dma((2, 2)), dma((2,)), dma,
     ]
     grad_tokens, grad_qkv, grad_out = pl.pallas_call(
         functools.partial(kernel, ny, nxh, nz, win, edge),

time: 82 us -> 79.6 us (0.971)
  Pallas kernels: 77.4 us -> 75.7 us
    pallas_call x1, Pallas kernels: 77.4 us -> 75.7 us  [on_device(): pl.pallas_call(functools.partial(kernel, ny, nxh, nz, win, edge), out_sha...]
where the time goes in v3:
time: 79.6 us; the launch traced here: 79.3 us
  Pallas kernels  75.7 us (95%)
  local copies, waits for them, and re-layouts  2.91 us (4%)
    pallas_call x1, Pallas kernels, on_device(): pl.pallas_call(functools.partial(kernel, ny, nxh, nz, win, edge), out_sha...  75.7 us
    unnamed x7, local copies, waits for them, and re-layouts  2.91 us

profile of v3, /device:TPU:1, one launch (start us, length us, event | category | flops | bytes accessed | tf_op | source)
XLA Modules:
  0.0 79.3 jit_solution(12904142896777435662)
XLA Ops:
  0.6 75.7 %shard_map.112 = (bf16[64,1024]{1,0:T(8,128)(2,1)}, f32[32,192]{1,0:T(8,128)}, f32[32,64]{1,0:T(8,128)}) custom-call(bf16[64,1024]{1,0:T(8,128)(2,1)} %tok_in.1, bf16[64,1024]{1,0:T(8,128)(2,1)} %cot_in.1, bf16[32,192]{1,0:T(8,128)(2,1)} %wq_in.1, bf16[32,64]{1,0:T(8,128)(2,1)} %bitcast.6, f32[1,1024]{1,0:T(1,128)} %bitcast.7, f32[1,1024]{1,0:T(1,128)} %bitcast.8, ...), custom_call_target="tpu_custom_call" | custom-call | tf_op jit(solution)/shard_map/pallas_call | solution.py:707
  76.4 0.0 copy-start
  76.4 1.6 %copy.15 = bf16[64,1024]{1,0:T(8,128)(2,1)} copy(bf16[64,1024]{1,0:T(8,128)(2,1)} %get-tuple-element.12) | data formatting | bytes 262144
  77.9 0.0 copy-done
  77.9 0.0 copy-start.1
  77.9 0.6 copy.16
  78.6 0.1 copy-done.1
  78.7 0.6 copy.17
Async XLA Ops:
  76.4 1.6 %copy-start = (f32[32,192]{1,0:T(8,128)S(1)}, f32[32,192]{1,0:T(8,128)}, u32[]{:S(2)}) copy-start(f32[32,192]{1,0:T(8,128)} %get-tuple-element.13) | copy-start | bytes 73732
  77.9 0.7 copy-start.1

commit v4 on v3

--- a/solution.py
+++ b/solution.py
@@ -225,38 +225,42 @@
         rows = pl.ds(pl.multiple_of((y % nyh) * blk + h * own, own), own)
         return copy(nrm.at[p], act.at[p, rows], f1s.at[p], f1r.at[h, p], sibling)
 
-    def ring(i, p, way):
-        rows = pl.ds(pl.multiple_of(i * blk, blk), blk)
+    def ring(i, p, h, way):
+        rows = pl.ds(pl.multiple_of(i * blk + h * own, own), own)
         return copy(
-            act.at[p, rows], act.at[p, rows], f2s.at[i, p, way], f2r.at[i, p], up if way == 0 else down
+            act.at[p, rows], act.at[p, rows], f2s.at[i, p, h, way], f2r.at[i, p, h],
+            up if way == 0 else down,
         )
 
     here = y % nyh
     for i in range(nyh):
         apart = (y + ny - i - nyh * c) % ny
         back = (ny - apart) % ny
-        pending.append((functools.partial(ring, i, 0, 0), apart < nyh))
-        pending.append((functools.partial(ring, i, 1, 0), apart < nyh - 1))
-        pending.append((functools.partial(ring, i, 1, 1), back < nyh))
-        pending.append((functools.partial(ring, i, 0, 1), back < nyh - 1))
-
-    for p in range(2):
         for h in range(2):
-
-            @pl.when(jnp.logical_and(half == c, jnp.logical_or(away, h != xl)))
+            pending.append((functools.partial(ring, i, 0, h, 0), apart < nyh))
+            pending.append((functools.partial(ring, i, 1, h, 0), apart < nyh - 1))
+            pending.append((functools.partial(ring, i, 1, h, 1), back < nyh))
+            pending.append((functools.partial(ring, i, 0, h, 1), back < nyh - 1))
+
+    for h in (xl, 1 - xl):
+        for p in range(2):
+            if h is xl:
+
+                @pl.when(jnp.logical_and(half == c, away))
+                def _():
+                    f1_in(h, p).wait_recv()
+
+            else:
+
+                @pl.when(half == c)
+                def _():
+                    f1_in(h, p).wait_recv()
+
+            @pl.when(half == c)
             def _():
-                f1_in(h, p).wait_recv()
-
-        @pl.when(half == c)
-        def _():
-            ring(here, p, p).start()
-
-    if nyh > 1:
-
-        @pl.when(half == c)
-        def _():
-            ring(here, 1, 0).start()
-            ring(here, 0, 1).start()
+                ring(here, p, h, p).start()
+                if nyh > 1:
+                    ring(here, p, h, 1 - p).start()
 
     def turn(i):
         rows = pl.ds(pl.multiple_of(i * blk, blk), blk)
@@ -340,31 +344,25 @@
         has_below = from_below < nyh
         has_above = from_above < nyh
 
-        @pl.when(has_below)
-        def _():
-            ring(from_below, 0, 0).wait_recv()
-            if t < nyh:
-                ring(from_below, 0, 0).start()
-
-        @pl.when(has_above)
-        def _():
-            ring(from_above, 1, 1).wait_recv()
-            if t < nyh:
-                ring(from_above, 1, 1).start()
+        def relay(i, p, h, way):
+            ring(i, p, h, way).wait_recv()
+            if t < (nyh if p == way else nyh - 1):
+                ring(i, p, h, way).start()
+
+        for h in (xl, 1 - xl):
+            for way_first in (True, False):
+                if t == nyh and not way_first:
+                    continue
+
+                @pl.when(has_below)
+                def _():
+                    relay(from_below, 0 if way_first else 1, h, 0)
+
+                @pl.when(has_above)
+                def _():
+                    relay(from_above, 1 if way_first else 0, h, 1)
 
         if t < nyh:
-
-            @pl.when(has_below)
-            def _():
-                ring(from_below, 1, 0).wait_recv()
-                if t < nyh - 1:
-                    ring(from_below, 1, 0).start()
-
-            @pl.when(has_above)
-            def _():
-                ring(from_above, 0, 1).wait_recv()
-                if t < nyh - 1:
-                    ring(from_above, 0, 1).start()
 
             @pl.when(has_above)
             def _():
@@ -698,7 +696,7 @@
         pltpu.VMEM((nz, 2, wr, 2 * HD), BF16),
         pltpu.VMEM((nz, 2, wr, 2 * HD), BF16),
         dma((9,)),
-        dma((2,)), dma((2, 2)), dma((nyh, 2, 2)), dma((nyh, 2)),
+        dma((2,)), dma((2, 2)), dma((nyh, 2, 2, 2)), dma((nyh, 2, 2)),
         dma((nz,)), dma((nz,)), dma((nxx,)), dma((nxx,)), dma, dma,
         dma((3,)), dma((2,)), dma((2,)), dma((2,)), dma((2, 2)), dma((2, 2)),
         dma((2,)), dma((2,)), dma((2, nxx)), dma((2, nxx)), dma((nz,)), dma((nz,)),

time: 79.6 us -> 77.7 us (0.976); the launches traced: 79.3 us -> 76.6 us
  Pallas kernels: 75.7 us -> 73 us
    pallas_call x1, Pallas kernels: 75.7 us -> 73 us  [on_device(): pl.pallas_call(functools.partial(kernel, ny, nxh, nz, win, edge), out_sha...]
where the time goes in v4:
time: 77.7 us; the launch traced here: 76.6 us
  Pallas kernels  73 us (94%)
  local copies, waits for them, and re-layouts  2.91 us (4%)
    pallas_call x1, Pallas kernels, on_device(): pl.pallas_call(functools.partial(kernel, ny, nxh, nz, win, edge), out_sha...  73 us
    unnamed x7, local copies, waits for them, and re-layouts  2.91 us

profile of v4, /device:TPU:1, one launch (start us, length us, event | category | flops | bytes accessed | tf_op | source)
XLA Modules:
  0.0 76.6 jit_solution(11859565610363199739)
XLA Ops:
  0.6 73.0 %shard_map.112 = (bf16[64,1024]{1,0:T(8,128)(2,1)}, f32[32,192]{1,0:T(8,128)}, f32[32,64]{1,0:T(8,128)}) custom-call(bf16[64,1024]{1,0:T(8,128)(2,1)} %tok_in.1, bf16[64,1024]{1,0:T(8,128)(2,1)} %cot_in.1, bf16[32,192]{1,0:T(8,128)(2,1)} %wq_in.1, bf16[32,64]{1,0:T(8,128)(2,1)} %bitcast.6, f32[1,1024]{1,0:T(1,128)} %bitcast.7, f32[1,1024]{1,0:T(1,128)} %bitcast.8, ...), custom_call_target="tpu_custom_call" | custom-call | tf_op jit(solution)/shard_map/pallas_call | solution.py:705
  73.6 0.0 copy-start
  73.6 1.6 %copy.15 = bf16[64,1024]{1,0:T(8,128)(2,1)} copy(bf16[64,1024]{1,0:T(8,128)(2,1)} %get-tuple-element.12) | data formatting | bytes 262144
  75.2 0.0 copy-done
  75.2 0.0 copy-start.1
  75.2 0.6 copy.16
  75.8 0.1 copy-done.1
  76.0 0.6 copy.17
Async XLA Ops:
  73.6 1.6 %copy-start = (f32[32,192]{1,0:T(8,128)S(1)}, f32[32,192]{1,0:T(8,128)}, u32[]{:S(2)}) copy-start(f32[32,192]{1,0:T(8,128)} %get-tuple-element.13) | copy-start | bytes 73732
  75.2 0.7 copy-start.1

commit v5 on v4

--- a/solution.py
+++ b/solution.py
@@ -33,6 +33,8 @@
     ns = nxh * nz * 2
     nyh = ny // 2
     nxx = 2 * nxh
+    z_far = sorted(range(1, nz), key=lambda j: -min(j, nz - j))
+    x_far = sorted(range(1, nxx), key=lambda j: -min(j, nxx - j))
     own = tok.shape[0]
     blk = 2 * own
     d_model = tok.shape[1]
@@ -210,7 +212,7 @@
         block = wbuf.at[xl, xh, (z + nz - j) % nz, c]
         return copy(block, block, wzs.at[j], wzr.at[j], z_peer(j))
 
-    for j in range(1, nz):
+    for j in z_far:
         launch(functools.partial(wz, j))
 
     def meta_out(n):
@@ -304,7 +306,7 @@
     def weights_x():
         for j in range(1, nz):
             wz_in(j).wait_recv()
-        for j in range(1, nxx):
+        for j in x_far:
             launch(functools.partial(wx, j))
 
     def weights_core():
@@ -492,18 +494,19 @@
         dc(q, 1 - c).wait_recv()
         for h in range(2):
             s2[q, h] = (dwf[q, h, :, :, c] + r1[q, h].astype(F32)).astype(BF16)
+        for j in x_far:
+            launch(functools.partial(dx, q, j))
+
+    def weights_total(q):
+        total = dwf[q, xl, xh, :, c] + r1[q, xl, xh].astype(F32)
         for j in range(1, nxx):
-            launch(functools.partial(dx, q, j))
+            dx(q, j).wait_recv()
+            total += r2[q, j].astype(F32)
+        tot[:, q] = total
+        s3[:, q] = total.astype(BF16)
 
     def weights_spread():
-        for q in (1, 0):
-            total = dwf[q, xl, xh, :, c] + r1[q, xl, xh].astype(F32)
-            for j in range(1, nxx):
-                dx(q, j).wait_recv()
-                total += r2[q, j].astype(F32)
-            tot[:, q] = total
-            s3[:, q] = total.astype(BF16)
-        for j in range(1, nz):
+        for j in z_far:
             launch(functools.partial(dz, j))
 
     weights_start(1, dot(xt[...], qab[...]))
@@ -536,31 +539,32 @@
     def own_out(h):
         return copy(osd.at[h], oself, oss.at[h], osr, at(y, h, xh, z, xl))
 
-    def chain_part(way, part, r):
+    def chain_piece(way, part, r, h):
         yy = (y + (r if way == 0 else ny - r)) % ny
         i = (yy + ny - nyh * c) % ny
         held = i < nyh
+
+        @pl.when(held)
+        def _():
+            total = pvf[i, h * own : (h + 1) * own, part * halfcol : (part + 1) * halfcol]
+            if r < hops(way, part):
+                chain_link(way, part, i, h).wait_recv()
+                total += crv[way, part, i, h].astype(F32)
+            csd[way, part, i, h] = total.astype(BF16)
+
+        if r > 1:
+            launch(functools.partial(chain_link, way, part, i, h), held)
+        else:
+            launch(functools.partial(chain_end, way, part, i, h, yy), held)
+
+    def chain(r):
         for h in range(2):
-
-            @pl.when(held)
-            def _():
-                total = pvf[i, h * own : (h + 1) * own, part * halfcol : (part + 1) * halfcol]
-                if r < hops(way, part):
-                    chain_link(way, part, i, h).wait_recv()
-                    total += crv[way, part, i, h].astype(F32)
-                csd[way, part, i, h] = total.astype(BF16)
-
-            if r > 1:
-                launch(functools.partial(chain_link, way, part, i, h), held)
-            else:
-                launch(functools.partial(chain_end, way, part, i, h, yy), held)
-
-    def chain(r):
-        for way in range(2):
-            chain_part(way, way, r)
+            for way in range(2):
+                chain_piece(way, way, r, h)
         if r > 1:
-            for way in range(2):
-                chain_part(way, 1 - way, r - 1)
+            for h in range(2):
+                for way in range(2):
+                    chain_piece(way, 1 - way, r - 1, h)
 
     for b in range(nyh):
         rows = pl.ds(b * blk, blk)
@@ -589,12 +593,14 @@
         oself[...] = osd[xl]
 
     weights_start(0, dot(xt[:, :win], gkvb[...]))
+    weights_cross(0)
     for r in range(nyh - 1, 0, -1):
         if r == 1:
+            weights_total(0)
             weights_spread()
         chain(r)
         if r == nyh - 1:
-            weights_cross(0)
+            weights_total(1)
 
     def owner_in(way, part):
         return copy(
@@ -644,7 +650,7 @@
     wide = 4 * HD
     dma = pltpu.SemaphoreType.DMA
     vmem = pl.BlockSpec(memory_space=pltpu.VMEM)
-    anywhere = pl.BlockSpec(memory_space=pl.ANY)
+    anywhere = pl.BlockSpec(memory_space=pltpu.MemorySpace.HBM)
     keys = win + edge
     blk = 2 * own
     scratch = [
@@ -712,10 +718,15 @@
         in_specs=[anywhere] * 9,
         out_specs=(vmem, vmem, vmem),
         scratch_shapes=scratch,
-        compiler_params=pltpu.CompilerParams(collective_id=0, has_side_effects=True),
+        compiler_params=pltpu.CompilerParams(collective_id=0, has_side_effects=True, vmem_limit_bytes=36 * 1024 * 1024),
     )(
-        tokens, cotangent, w_qkv, w_out.T,
-        mod_scale[None, :], mod_shift[None, :], mod_gate[None, :], counts, edge_index,
+        *(
+            pltpu.with_memory_space_constraint(a, pltpu.MemorySpace.HBM)
+            for a in (
+                tokens, cotangent, w_qkv, w_out.T,
+                mod_scale[None, :], mod_shift[None, :], mod_gate[None, :], counts, edge_index,
+            )
+        )
     )
     return (grad_tokens, grad_qkv, grad_out.T)
 

time: 77.7 us -> 75.9 us (0.977)
  local copies, waits for them, and re-layouts: 2.91 us -> 1.88 us
  Pallas kernels: 73 us -> 72.1 us
    unnamed x7 -> x3, local copies, waits for them, and re-layouts: 2.91 us -> 1.88 us
    pallas_call x1, Pallas kernels: 73 us -> 72.1 us  [on_device(): pl.pallas_call(functools.partial(kernel, ny, nxh, nz, win, edge), out_sha...]
where the time goes in v5:
time: 75.9 us; the launch traced here: 74.7 us
  Pallas kernels  72.1 us (95%)
  local copies, waits for them, and re-layouts  1.88 us (2%)
    pallas_call x1, Pallas kernels, on_device(): pl.pallas_call(functools.partial(kernel, ny, nxh, nz, win, edge), out_sha...  72.1 us
    unnamed x3, local copies, waits for them, and re-layouts  1.88 us

profile of v5, /device:TPU:1, one launch (start us, length us, event | category | flops | bytes accessed | tf_op | source)
XLA Modules:
  0.0 74.7 jit_solution(15426522462970714419)
XLA Ops:
  0.6 72.1 %shard_map.112 = (bf16[64,1024]{1,0:T(8,128)(2,1)S(1)}, f32[32,192]{1,0:T(8,128)S(1)}, f32[32,64]{1,0:T(8,128)S(1)}) custom-call(bf16[64,1024]{1,0:T(8,128)(2,1)} %tok_in.1, bf16[64,1024]{1,0:T(8,128)(2,1)} %cot_in.1, bf16[32,192]{1,0:T(8,128)(2,1)} %wq_in.1, bf16[32,64]{1,0:T(8,128)(2,1)} %bitcast.6, f32[1,1024]{1,0:T(1,128)} %bitcast.7, ...), custom_call_target="tpu_custom_call" | custom-call | tf_op jit(solution)/shard_map/pallas_call | solution.py:711
  72.8 0.7 copy.15
  73.4 0.6 copy.16
  74.1 0.6 copy.17

commit v6 on v5

--- a/solution.py
+++ b/solution.py
@@ -279,7 +279,9 @@
             w = wbuf[h].reshape(d_model, 4 * HD)
             from_normed = dot(act[0, rows, :], w)
             from_upstream = dot(act[1, rows, :], w[:, 2 * HD :])
-            kv[h, rows, :] = from_normed[:, : 2 * HD].astype(BF16)
+            pair = from_normed[:, : 2 * HD].astype(BF16)
+            kv[h, rows, :] = pair
+            kvt[h, :, rows] = pair.T
             query = from_normed[:, 2 * HD :].astype(BF16).astype(F32) * (HD**-0.5)
             qa[h, 0, rows, :] = jnp.where(lane < HD, query, 0.0).astype(BF16)
             qa[h, 1, rows, :] = jnp.where(
@@ -323,24 +325,34 @@
 
         meta_out(1).wait_recv()
 
-    def far(i):
-        return (y + ny - i - nyh * c) % ny == nyh
+    def hot():
+        row_id = lax.broadcasted_iota(jnp.int32, (win, edge), 0) + c * win
+        for k in range(2):
+            hit = row_id == meta_next[k : k + 1, :]
+            oh[:, k * edge : (k + 1) * edge] = hit.astype(F32).astype(BF16)
+
+    def project_near(t):
+        @pl.loop(0, nyh)
+        def _(i):
+            apart = (y + ny - i - nyh * c) % ny
+
+            @pl.when(jnp.minimum(apart, ny - apart) < t)
+            def _():
+                project(i)
 
     stages = [weights_x, weights_core, weights_done]
+    ready = False
     for t in range(1, nyh + 1):
-        if t == nyh:
-            for stage in stages:
-                stage()
-            stages = []
-
-            @pl.loop(0, nyh)
-            def _(i):
-                @pl.when(jnp.logical_not(far(i)))
-                def _():
-                    project(i)
-
-        elif stages:
+        if stages:
             stages.pop(0)()
+            if t == nyh:
+                for stage in stages:
+                    stage()
+                stages = []
+            if not stages:
+                hot()
+                project_near(t)
+                ready = True
         from_below = (y + 2 * ny - t - nyh * c) % ny
         from_above = (y + 2 * ny + t - nyh * c) % ny
         has_below = from_below < nyh
@@ -368,32 +380,35 @@
 
             @pl.when(has_above)
             def _():
+                if ready:
+                    project(from_above)
                 turn(from_above)
 
         @pl.when(has_below)
         def _():
-            turn(from_below)
-            if t == nyh:
+            if ready:
                 project(from_below)
-
-    row_id = lax.broadcasted_iota(jnp.int32, (win, edge), 0) + c * win
-    for k in range(2):
-        oh[:, k * edge : (k + 1) * edge] = (row_id == meta_next[k : k + 1, :]).astype(F32).astype(BF16)
-    for h in range(2):
-        kvt[h, :, :win] = kv[h, :win, :].T
+            if t < nyh:
+                turn(from_below)
+
+    def edge_out(h, k):
+        return copy(e_send.at[h, k], e_recv.at[h, c], es.at[h, k], er.at[h, c], at_slab(after, k))
+
+    def edge_in(h, k):
+        return copy(e_send.at[h, k], e_recv.at[h, k], es.at[h, k], er.at[h, k], sibling)
+
     for h in range(2):
         picked = dot(kvt[h, :, :win], oh[...]).astype(BF16)
         for k in range(2):
-            e_send[k, h] = picked[:, k * edge : (k + 1) * edge]
-
-    def edge_out(k):
-        return copy(e_send.at[k], e_recv.at[c], es.at[k], er.at[c], at_slab(after, k))
-
-    def edge_in(k):
-        return copy(e_send.at[k], e_recv.at[k], es.at[k], er.at[k], sibling)
-
-    for k in range(2):
-        launch(functools.partial(edge_out, k))
+            e_send[h, k] = picked[:, k * edge : (k + 1) * edge]
+            launch(functools.partial(edge_out, h, k))
+
+    last = (y + ny - nyh - nyh * c) % ny
+
+    @pl.when(last < nyh)
+    def _():
+        turn(last)
+
     keys = win + edge
     step = 256 if win % 256 == 0 else win
     has_edge = mine > 0
@@ -417,14 +432,13 @@
             stat[h, 1:2, q_rows] = jnp.sum(exponent, 0, keepdims=True)
             stat[h, 2:3, q_rows] = jnp.sum(exponent * g_prob, 0, keepdims=True)
 
-    for k in range(2):
-        edge_in(k).wait_recv()
-    for h in range(2):
-        arrived = e_recv[0, h].astype(F32) + e_recv[1, h].astype(F32)
+    def scores_of(h):
+        for k in range(2):
+            edge_in(h, k).wait_recv()
+        arrived = e_recv[h, 0].astype(F32) + e_recv[h, 1].astype(F32)
         kvt[h, :, win:] = arrived.astype(BF16)
         kv[h, win:, :] = arrived.T.astype(BF16)
 
-    def scores_of(h):
         @pl.loop(0, win // step)
         def _(n):
             q_rows = pl.ds(pl.multiple_of(n * step, step), step)
@@ -637,6 +651,17 @@
     out_o[...] = final[1, :, HD:]
 
     drain()
+
+
+def write_out(tok, qkv, o, out_tok, out_qkv, out_o, sems):
+    moves = [
+        pltpu.make_async_copy(src, dst, sems.at[n])
+        for n, (src, dst) in enumerate(((tok, out_tok), (qkv, out_qkv), (o, out_o)))
+    ]
+    for move in moves:
+        move.start()
+    for move in moves:
+        move.wait()
 
 
 def on_device(nxh, tokens, cotangent, w_qkv, w_out, mod_scale, mod_shift, mod_gate, counts, edge_index):
@@ -704,7 +729,7 @@
         dma((9,)),
         dma((2,)), dma((2, 2)), dma((nyh, 2, 2, 2)), dma((nyh, 2, 2)),
         dma((nz,)), dma((nz,)), dma((nxx,)), dma((nxx,)), dma, dma,
-        dma((3,)), dma((2,)), dma((2,)), dma((2,)), dma((2, 2)), dma((2, 2)),
+        dma((3,)), dma((2,)), dma((2, 2)), dma((2, 2)), dma((2, 2)), dma((2, 2)),
         dma((2,)), dma((2,)), dma((2, nxx)), dma((2, nxx)), dma((nz,)), dma((nz,)),
         dma((2, 2, nyh, 2)), dma((2, 2, nyh, 2)), dma((2, 2, 2)), dma((2, 2)), dma((2,)), dma,
     ]
@@ -728,6 +753,14 @@
             )
         )
     )
+    grad_tokens, grad_qkv, grad_out = pl.pallas_call(
+        write_out,
+        out_shape=tuple(jax.ShapeDtypeStruct(a.shape, a.dtype) for a in (grad_tokens, grad_qkv, grad_out)),
+        in_specs=[vmem] * 3,
+        out_specs=(anywhere,) * 3,
+        scratch_shapes=[dma((3,))],
+        compiler_params=pltpu.CompilerParams(vmem_limit_bytes=4 * 1024 * 1024),
+    )(grad_tokens, grad_qkv, grad_out)
     return (grad_tokens, grad_qkv, grad_out.T)
 
 

time: 75.9 us -> 73.8 us (0.972)
  local copies, waits for them, and re-layouts: 1.88 us -> 0 us
    unnamed x3 -> x0, local copies, waits for them, and re-layouts: 1.88 us -> none
    pallas_call x1, Pallas kernels: 72.1 us -> 71.1 us  [on_device(): pl.pallas_call(functools.partial(kernel, ny, nxh, nz, win, edge), out_sha...]
where the time goes in v6:
time: 73.8 us; the launch traced here: 72.4 us
  Pallas kernels  71.8 us (97%)
    pallas_call x1, Pallas kernels, on_device(): pl.pallas_call(functools.partial(kernel, ny, nxh, nz, win, edge), out_sha...  71.1 us

profile of v6, /device:TPU:1, one launch (start us, length us, event | category | flops | bytes accessed | tf_op | source)
XLA Modules:
  0.0 72.4 jit_solution(11011749460048375492)
XLA Ops:
  0.6 71.1 %shard_map.112 = (bf16[64,1024]{1,0:T(8,128)(2,1)S(1)}, f32[32,192]{1,0:T(8,128)S(1)}, f32[32,64]{1,0:T(8,128)S(1)}) custom-call(bf16[64,1024]{1,0:T(8,128)(2,1)} %tok_in.1, bf16[64,1024]{1,0:T(8,128)(2,1)} %cot_in.1, bf16[32,192]{1,0:T(8,128)(2,1)} %wq_in.1, bf16[32,64]{1,0:T(8,128)(2,1)} %bitcast.5, f32[1,1024]{1,0:T(1,128)} %bitcast.6, ...), custom_call_target="tpu_custom_call" | custom-call | tf_op jit(solution)/shard_map/pallas_call | solution.py:736
  71.7 0.7 shard_map.113

commit v7 on v6

--- a/solution.py
+++ b/solution.py
@@ -533,7 +533,6 @@
         returned = dot(oh[...], g_recv[h].reshape(2 * edge, 2 * HD))
         gkvb[:, cols] = (own_pair + returned).astype(BF16)
 
-    weights_cross(1)
 
     def hops(way, part):
         return nyh if way == part else nyh - 1
@@ -580,14 +579,15 @@
                 for way in range(2):
                     chain_piece(way, 1 - way, r - 1, h)
 
-    for b in range(nyh):
-        rows = pl.ds(b * blk, blk)
-        total = jnp.zeros((blk, d_model), F32)
-        for h in range(2):
-            cols = pl.ds(h * 2 * HD, 2 * HD)
-            both = jnp.concatenate([gkvb[rows, cols], qab[rows, cols]], 1)
-            total += dot(both, wbuf[h].reshape(d_model, 4 * HD), ((1,), (1,)))
-        pvf[b] = total
+    grads = jnp.concatenate(
+        [gkvb[:, : 2 * HD], qab[:win, : 2 * HD], gkvb[:, 2 * HD :], qab[:win, 2 * HD :]], 1
+    )
+    flat = [wbuf[h].reshape(d_model, 4 * HD) for h in range(2)]
+    width = halfcol // 2
+    for n in range(4):
+        cols = slice(n * width, (n + 1) * width)
+        both = jnp.concatenate([w[cols, :] for w in flat], 1)
+        pvf[:, :, cols] = dot(grads, both, ((1,), (1,))).reshape(nyh, blk, width)
 
     chain(nyh)
 
@@ -607,6 +607,7 @@
         oself[...] = osd[xl]
 
     weights_start(0, dot(xt[:, :win], gkvb[...]))
+    weights_cross(1)
     weights_cross(0)
     for r in range(nyh - 1, 0, -1):
         if r == 1:

time: 73.8 us -> 73 us (0.989)
  Pallas kernels: 71.8 us -> 71 us
    pallas_call x1, Pallas kernels: 71.1 us -> 70.3 us  [on_device(): pl.pallas_call(functools.partial(kernel, ny, nxh, nz, win, edge), out_sha...]
where the time goes in v7:
time: 73 us; the launch traced here: 71.6 us
  Pallas kernels  71 us (97%)
    pallas_call x1, Pallas kernels, on_device(): pl.pallas_call(functools.partial(kernel, ny, nxh, nz, win, edge), out_sha...  70.3 us

profile of v7, /device:TPU:1, one launch (start us, length us, event | category | flops | bytes accessed | tf_op | source)
XLA Modules:
  0.0 71.6 jit_solution(1031267860969622953)
XLA Ops:
  0.6 70.3 %shard_map.112 = (bf16[64,1024]{1,0:T(8,128)(2,1)S(1)}, f32[32,192]{1,0:T(8,128)S(1)}, f32[32,64]{1,0:T(8,128)S(1)}) custom-call(bf16[64,1024]{1,0:T(8,128)(2,1)} %tok_in.1, bf16[64,1024]{1,0:T(8,128)(2,1)} %cot_in.1, bf16[32,192]{1,0:T(8,128)(2,1)} %wq_in.1, bf16[32,64]{1,0:T(8,128)(2,1)} %bitcast.5, f32[1,1024]{1,0:T(1,128)} %bitcast.6, ...), custom_call_target="tpu_custom_call" | custom-call | tf_op jit(solution)/shard_map/pallas_call | solution.py:737
  70.9 0.7 shard_map.113

commit v8 on v7

--- a/solution.py
+++ b/solution.py
@@ -101,18 +101,30 @@
                 def _():
                     make().wait_send()
 
+    arrivals = [
+        pltpu.make_async_copy(src, dst, ins.at[n])
+        for n, (src, dst) in enumerate(
+            (
+                (tok_in, tok), (cot_in, cot), (wq_in, wq), (wo_in, wo), (scale_in, scale),
+                (shift_in, shift), (gate_in, gate), (counts_in, counts), (edges_in, edges),
+            )
+        )
+    ]
+    for arrival in arrivals:
+        arrival.start()
+
     barrier = pltpu.get_barrier_semaphore()
 
     def greet(to):
         pl.semaphore_signal(barrier, inc=1, device_id=to, device_id_type=MESH)
 
-    greet(sibling)
+    for j in z_far:
+        greet(z_peer(j))
+    for j in x_far:
+        greet(x_peer(j))
     greet(up)
     greet(down)
-    for j in range(1, nz):
-        greet(z_peer(j))
-    for j in range(1, nxx):
-        greet(x_peer(j))
+    greet(sibling)
     for k in range(2):
         greet(at_slab(after, k))
         greet(at_slab(before, k))
@@ -144,17 +156,6 @@
         + 2 * count_of(below // nyh == c)
     )
 
-    arrivals = [
-        pltpu.make_async_copy(src, dst, ins.at[n])
-        for n, (src, dst) in enumerate(
-            (
-                (tok_in, tok), (cot_in, cot), (wq_in, wq), (wo_in, wo), (scale_in, scale),
-                (shift_in, shift), (gate_in, gate), (counts_in, counts), (edges_in, edges),
-            )
-        )
-    ]
-    for arrival in arrivals:
-        arrival.start()
     for arrival in arrivals:
         arrival.wait()
 

time: 73 us -> 73.7 us (level)
  the two profiles are of different devices: /device:TPU:1 before, /device:TPU:2 now
where the time goes in v8:
time: 73.7 us; the launch traced here: 73.6 us
  Pallas kernels  72.9 us (99%)
    pallas_call x1, Pallas kernels, on_device(): pl.pallas_call(functools.partial(kernel, ny, nxh, nz, win, edge), out_sha...  72.2 us

profile of v8, /device:TPU:2, one launch (start us, length us, event | category | flops | bytes accessed | tf_op | source)
XLA Modules:
  0.0 73.6 jit_solution(3075784707297129082)
XLA Ops:
  0.6 72.2 %shard_map.112 = (bf16[64,1024]{1,0:T(8,128)(2,1)S(1)}, f32[32,192]{1,0:T(8,128)S(1)}, f32[32,64]{1,0:T(8,128)S(1)}) custom-call(bf16[64,1024]{1,0:T(8,128)(2,1)} %tok_in.1, bf16[64,1024]{1,0:T(8,128)(2,1)} %cot_in.1, bf16[32,192]{1,0:T(8,128)(2,1)} %wq_in.1, bf16[32,64]{1,0:T(8,128)(2,1)} %bitcast.5, f32[1,1024]{1,0:T(1,128)} %bitcast.6, ...), custom_call_target="tpu_custom_call" | custom-call | tf_op jit(solution)/shard_map/pallas_call | solution.py:738
  72.9 0.7 shard_map.113
